TPU v7x, 32 devices: a whole 2x2x4 slice. The times are simulated.
32 devices in a mesh: shard: 8 (over y, x, core), tp: 4 (over z).
Axes of the slice: x: 2, y: 2, z: 4, core: 2. Of those that a mesh axis runs over, the one named last changes fastest.
Arguments:
- weight_gate: bfloat16 [2560, 9728], P('shard', 'tp'), may hold values from -0.15625 to 0.15625
- low_gate: bfloat16 [2560, 32], P('shard'), may hold values from -0.125 to 0.125
- high_gate: bfloat16 [32, 9728], P(None, 'tp'), may hold values from -1 to 1
- weight_up: bfloat16 [2560, 9728], P('shard', 'tp'), may hold values from -0.15625 to 0.15625
- low_up: bfloat16 [2560, 32], P('shard'), may hold values from -0.125 to 0.125
- high_up: bfloat16 [32, 9728], P(None, 'tp'), may hold values from -1 to 1
- norm_gain: float32 [2560], P('shard'), may hold values from 0.25 to 1.75
Outputs:
- ready_gate: bfloat16 [2560, 9728], P(None, 'tp')
- ready_up: bfloat16 [2560, 9728], P(None, 'tp')
- factor_gate: float32 [9728], P('tp')
- factor_up: float32 [9728], P('tp')
All inputs are finite; a program needn't handle non-finite values.
Results may differ from a plain program's by a relative error of at most 0.001.
Values may be sent and summed in bfloat16 or wider, within the bound.
A program may use at most 128 MiB of HBM per device.

v0:
```python
import functools
import math

import jax
import jax.numpy as jnp
from jax import lax
from jax.experimental import pallas as pl
from jax.experimental.pallas import tpu as pltpu
from jax.sharding import PartitionSpec as P

mix_rate = 2.0
AXIS = "shard"


def local(weight_gate, low_gate, high_gate, weight_up, low_up, high_up, norm_gain):
    latest_gate = weight_gate.astype(jnp.float32) + mix_rate * jnp.dot(
        low_gate, high_gate, preferred_element_type=jnp.float32
    )
    latest_up = weight_up.astype(jnp.float32) + mix_rate * jnp.dot(
        low_up, high_up, preferred_element_type=jnp.float32
    )
    latest_gained_gate = latest_gate * norm_gain[:, None]
    latest_gained_up = latest_up * norm_gain[:, None]
    total_gate, total_up = lax.psum(
        (
            jnp.sum(latest_gained_gate * latest_gained_gate, axis=0),
            jnp.sum(latest_gained_up * latest_gained_up, axis=0),
        ),
        AXIS,
    )
    factor_gate = jnp.sqrt(total_gate)
    factor_up = jnp.sqrt(total_up)
    narrow_gate = (latest_gained_gate / factor_gate).astype(jnp.bfloat16)
    narrow_up = (latest_gained_up / factor_up).astype(jnp.bfloat16)
    ready_gate = lax.all_gather(narrow_gate, AXIS, axis=0, tiled=True)
    ready_up = lax.all_gather(narrow_up, AXIS, axis=0, tiled=True)
    return (ready_gate, ready_up, factor_gate, factor_up)


def gather_kernel(
    n, chunks, raw, wg_hbm, wu_hbm, lg_hbm, lu_hbm, hg_hbm, hu_hbm, gain_hbm,
    out_g, out_u, fac,
    w_v, l_v, h_v, gain_v, low_v, g_v, col_v, sums, rf_v, far_low,
    in_sem, ssum, rsum, slow, rlow, send, recv,
):
    rows, cols = wg_hbm.shape
    step = rows // chunks
    me = lax.axis_index(AXIS)
    core = lax.rem(me, 2)
    x = lax.rem(me // 2, 2)
    y = me // 4
    sib = me + 1 - 2 * core
    to_x = me + 2 - 4 * x
    to_y = me + 4 - 8 * y
    diag = to_x + 4 - 8 * y

    barrier = pltpu.get_barrier_semaphore()
    for d in range(1, n):
        pl.semaphore_signal(barrier, inc=1, device_id={AXIS: lax.rem(me + d, n)})

    gain_load = pltpu.make_async_copy(gain_hbm, gain_v, in_sem.at[6])
    low_loads, high_loads, loads = (
        [
            pltpu.make_async_copy(src, dst.at[a], in_sem.at[3 * a + i])
            for a, src in enumerate(pair)
        ]
        for i, (pair, dst) in enumerate((
            ((lg_hbm, lu_hbm), l_v), ((hg_hbm, hu_hbm), h_v), ((wg_hbm, wu_hbm), w_v)
        ))
    )
    gain_load.start()
    for a in range(2):
        for c in (low_loads[a], high_loads[a], loads[a]):
            c.start()

    early = raw * step
    outs = (out_g, out_u)
    every = [(a, k) for a in range(2) for k in range(chunks)]
    started = {}

    def move(slot, a, k, owner, target, base=None):
        r = pl.ds(pl.multiple_of(owner * rows + k * step, 16), step)
        part = outs[a].at[r, :]
        return pltpu.make_async_remote_copy(
            src_ref=part if base is None else base.at[k * step:(k + 1) * step, :],
            dst_ref=part,
            send_sem=send.at[slot, a * chunks + k], recv_sem=recv.at[slot, a * chunks + k],
            device_id={AXIS: target})

    def go(*args):
        started[args[:3]] = move(*args)
        started[args[:3]].start()

    def send_own(a, k):
        go(0, a, k, me, to_x)
        go(1, a, k, me, to_y)
        go(2, a, k, me, sib)

    def send_raw(a, k):
        go(0, a, k, me, to_x, wg_hbm)
        go(1, a, k, me, to_y, wg_hbm)
        go(2, a, k, me, sib, wg_hbm)

    pl.semaphore_wait(barrier, n - 1)
    send_raw(0, 0)

    gain_load.wait()
    col_v[...] = jnp.broadcast_to(gain_v[...], (128, rows)).T
    for a in range(2):
        low_loads[a].wait()
        low_v[a] = (mix_rate * l_v[a].astype(jnp.float32)).T.astype(jnp.bfloat16)
        high_loads[a].wait()
        loads[a].wait()
        acc = jnp.zeros((8, cols), jnp.float32)
        for k in range(chunks):
            r = pl.ds(k * step, step)
            prod = jnp.dot(low_v[a, r, :], h_v[a], preferred_element_type=jnp.float32)
            new = (w_v[a, r, :].astype(jnp.float32) + prod) * col_v[r, 0:1]
            g_v[a, r, :] = new
            acc = acc + jnp.sum((new * new).reshape(step // 8, 8, cols), axis=0)
        sums[me, :, a * cols:(a + 1) * cols] = jnp.sum(acc, axis=0, keepdims=True)

    sums[me, :, 2 * cols:] = gain_v[:, :early]
    shares = []
    for d in range(1, n):
        shares.append(pltpu.make_async_remote_copy(
            src_ref=sums.at[me], dst_ref=sums.at[me],
            send_sem=ssum.at[d], recv_sem=rsum.at[d],
            device_id={AXIS: lax.rem(me + d, n)}))
        shares[-1].start()
    lows = []
    for d in range(1, n):
        lows.append(pltpu.make_async_remote_copy(
            src_ref=l_v.at[0, :, :early], dst_ref=far_low.at[me],
            send_sem=slow.at[d], recv_sem=rlow.at[d],
            device_id={AXIS: lax.rem(me + d, n)}))
        lows[-1].start()
    for k in range(1, raw):
        send_raw(0, k)
    for c in shares:
        c.wait_recv()
    total = sums[0, :, :2 * cols]
    for d in range(1, n):
        total = total + sums[d, :, :2 * cols]
    factor = jnp.sqrt(total)
    fac[...] = factor
    rf_v[...] = 1.0 / factor

    for i, (a, k) in enumerate(every):
        new = g_v[a, k * step:(k + 1) * step, :] * rf_v[:, a * cols:(a + 1) * cols]
        r = pl.ds(pl.multiple_of(me * rows + k * step, 16), step)
        outs[a][r, :] = new.astype(jnp.bfloat16)
        if i > raw:
            send_own(*every[i - 1])
    send_own(*every[-1])

    for i, (a, k) in enumerate(every):
        move(0, a, k, to_x, to_x).wait_recv()
        if i % 2 == 0:
            go(5, a, k, to_x, to_y)
        go(3, a, k, to_x, sib)
        move(1, a, k, to_y, to_y).wait_recv()
        if i % 2 == 1:
            go(5, a, k, to_y, to_x)
        go(4, a, k, to_y, sib)

    flip = 1 - 2 * core

    def from_sib(a, k):
        move(2, a, k, sib, sib).wait_recv()
        move(3, a, k, to_x + flip, sib).wait_recv()
        move(4, a, k, to_y + flip, sib).wait_recv()
        move(6, a, k, diag + flip, sib).wait_recv()

    def finish_raw():
        for a, k in every[:raw]:
            from_sib(a, k)
            for slot in (3, 4, 5, 6):
                started.pop((slot, a, k)).wait_send()
        for c in lows:
            c.wait_recv()

        @pl.loop(1, n)
        def _(d):
            owner = lax.rem(me + d, n)
            low = (mix_rate * far_low[owner].astype(jnp.float32)).T.astype(jnp.bfloat16)
            col = jnp.broadcast_to(sums[owner, :, 2 * cols:], (128, early)).T[:, 0:1]
            r = pl.ds(pl.multiple_of(owner * rows, 16), early)
            prod = jnp.dot(low, h_v[0], preferred_element_type=jnp.float32)
            new = (out_g[r, :].astype(jnp.float32) + prod) * col
            out_g[r, :] = (new * rf_v[:, :cols]).astype(jnp.bfloat16)

    for i, (a, k) in enumerate(every):
        if i == 3 * raw:
            finish_raw()
        move(5, a, k, diag, to_x).wait_recv()
        go(6, a, k, diag, sib)
    for a, k in every[raw:]:
        from_sib(a, k)
    for c in started.values():
        c.wait_send()
    for c in shares + lows:
        c.wait_send()


def write_kernel(parts, a_v, b_v, a_hbm, b_hbm, sem):
    step = a_v.shape[0] // parts
    copies = []
    for i, (src, dst) in enumerate(((a_v, a_hbm), (b_v, b_hbm))):
        for k in range(parts):
            r = pl.ds(k * step, step)
            copies.append(pltpu.make_async_copy(src.at[r, :], dst.at[r, :], sem.at[i, k]))
    for c in copies:
        c.start()
    for c in copies:
        c.wait()


def paired(n, weight_gate, low_gate, high_gate, weight_up, low_up, high_up, norm_gain):
    rows, cols = weight_gate.shape
    chunks, raw = 5, 2
    early = raw * rows // chunks
    full = (n * rows, cols)
    vmem = pl.BlockSpec(memory_space=pltpu.VMEM)
    hbm = pl.BlockSpec(memory_space=pl.ANY)
    gain = norm_gain.reshape(1, rows)
    space = pl.BlockSpec(memory_space=pltpu.HBM)
    rank = high_gate.shape[0]
    grant = 65472 * 2**10 - (4 * full[0] * cols + 8 * cols) // 2**10 * 2**10 - 24 * 2**10
    gate, up, fac = pl.pallas_call(
        functools.partial(gather_kernel, n, chunks, raw),
        out_shape=(
            pltpu.VMEM(full, jnp.bfloat16),
            pltpu.VMEM(full, jnp.bfloat16),
            jax.ShapeDtypeStruct((1, 2 * cols), jnp.float32),
        ),
        in_specs=[space] * 7,
        out_specs=(vmem, vmem, vmem),
        scratch_shapes=[
            pltpu.VMEM((2, rows, cols), jnp.bfloat16),
            pltpu.VMEM((2, rank, rows), jnp.bfloat16),
            pltpu.VMEM((2, rank, cols), jnp.bfloat16),
            pltpu.VMEM((1, rows), jnp.float32),
            pltpu.VMEM((2, rows, rank), jnp.bfloat16),
            pltpu.VMEM((2, rows, cols), jnp.float32),
            pltpu.VMEM((rows, 128), jnp.float32),
            pltpu.VMEM((n, 1, 2 * cols + early), jnp.float32),
            pltpu.VMEM((1, 2 * cols), jnp.float32),
            pltpu.VMEM((n, rank, early), jnp.bfloat16),
            pltpu.SemaphoreType.DMA((7,)),
            pltpu.SemaphoreType.DMA((n,)),
            pltpu.SemaphoreType.DMA((n,)),
            pltpu.SemaphoreType.DMA((n,)),
            pltpu.SemaphoreType.DMA((n,)),
            pltpu.SemaphoreType.DMA((7, 2 * chunks)),
            pltpu.SemaphoreType.DMA((7, 2 * chunks)),
        ],
        compiler_params=pltpu.CompilerParams(
            collective_id=0, has_side_effects=True, vmem_limit_bytes=grant
        ),
        name="merge_gather",
    )(weight_gate, weight_up, low_gate.T, low_up.T, high_gate, high_up, gain)
    parts = 8
    ready_gate, ready_up = pl.pallas_call(
        functools.partial(write_kernel, parts),
        out_shape=(jax.ShapeDtypeStruct(full, jnp.bfloat16),) * 2,
        in_specs=[vmem, vmem],
        out_specs=(hbm, hbm),
        scratch_shapes=[pltpu.SemaphoreType.DMA((2, parts))],
        compiler_params=pltpu.CompilerParams(vmem_limit_bytes=2**20),
        name="write_out",
    )(gate, up)
    return ready_gate, ready_up, fac[0, :cols], fac[0, cols:]


def solution(mesh):
    in_specs = (
        P("shard", "tp"),
        P("shard", None),
        P(None, "tp"),
        P("shard", "tp"),
        P("shard", None),
        P(None, "tp"),
        P("shard"),
    )
    out_specs = (P(None, "tp"), P(None, "tp"), P("tp"), P("tp"))
    n = mesh.shape[AXIS]
    side = math.isqrt(n // 2)
    body = functools.partial(paired, n) if side == 2 and 2 * side * side == n else local
    return jax.shard_map(body, mesh=mesh, in_specs=in_specs, out_specs=out_specs, check_vma=False)
```

profile of v0, /device:TPU:0, one launch (start us, length us, event | category | flops | bytes accessed | tf_op | source)
XLA Modules:
  0.0 123.1 jit_solution(13026275068431772518)
XLA Ops:
  0.6 1.2 %reshape.11.gain_hbm = f32[1,320]{1,0:T(1,128)} reshape(f32[320]{0:T(512)} %param.13) | data formatting | bytes 2560 | tf_op jit(solution)/shard_map/reshape | solution.py:226
  1.9 112.1 %merge_gather.1 = (bf16[2560,2432]{1,0:T(8,128)(2,1)S(1)}, bf16[2560,2432]{1,0:T(8,128)(2,1)S(1)}, f32[1,4864]{1,0:T(1,128)}) custom-call(bf16[320,2432]{1,0:T(8,128)(2,1)} %wg_hbm.1, bf16[320,2432]{1,0:T(8,128)(2,1)} %wu_hbm.1, bf16[32,320]{1,0:T(8,128)(2,1)} %bitcast.2, bf16[32,320]{1,0:T(8,128)(2,1)} %bitcast.3, bf16[32,2432]{1,0:T(8,128)(2,1)} %hg_hbm.1, ...), custom_call_target="tpu_custom_call" | custom-call | tf_op jit(solution)/shard_map/merge_gather/pallas_call | solution.py:230
  114.0 0.0 copy-start
  114.0 8.4 %write_out.1 = (bf16[2560,2432]{1,0:T(8,128)(2,1)}, bf16[2560,2432]{1,0:T(8,128)(2,1)}) custom-call(bf16[2560,2432]{1,0:T(8,128)(2,1)S(1)} %get-tuple-element.9.a_v, bf16[2560,2432]{1,0:T(8,128)(2,1)S(1)} %get-tuple-element.10.b_v), custom_call_target="tpu_custom_call" | custom-call | tf_op jit(solution)/shard_map/write_out/pallas_call | solution.py:264
  122.4 0.0 copy-done
  122.4 0.6 slice_reduce_fusion
Async XLA Ops:
  114.0 8.5 %copy-start = (f32[1,4864]{1,0:T(1,128)S(1)}, f32[1,4864]{1,0:T(1,128)}, u32[]{:S(2)}) copy-start(f32[1,4864]{1,0:T(1,128)} %get-tuple-element.13) | copy-start | bytes 58372
where the time goes:
time: 123 us
  Pallas kernels  121 us (98%)
  local copies, waits for them, and re-layouts  1.9 us (2%)
    pallas_call x1, Pallas kernels, paired(): pl.pallas_call(functools.partial(gather_kernel, n, chunks, raw), out_shap...  112 us
    pallas_call x1, Pallas kernels, paired(): pl.pallas_call(functools.partial(write_kernel, parts), out_shape=(jax.Sha...  8.43 us

commit v1 on v0

--- a/solution.py
+++ b/solution.py
@@ -58,7 +58,7 @@
     for d in range(1, n):
         pl.semaphore_signal(barrier, inc=1, device_id={AXIS: lax.rem(me + d, n)})
 
-    gain_load = pltpu.make_async_copy(gain_hbm, gain_v, in_sem.at[6])
+    gain_load = pltpu.make_async_copy(gain_hbm, gain_v.at[0], in_sem.at[6])
     low_loads, high_loads, loads = (
         [
             pltpu.make_async_copy(src, dst.at[a], in_sem.at[3 * a + i])
@@ -203,9 +203,13 @@
         c.wait_send()
 
 
-def write_kernel(parts, a_v, b_v, a_hbm, b_hbm, sem):
-    step = a_v.shape[0] // parts
-    copies = []
+def write_kernel(parts, a_v, b_v, fac, a_hbm, b_hbm, fa_hbm, fb_hbm, sem, fac_sem):
+    rows, cols = a_v.shape
+    step = rows // parts
+    copies = [
+        pltpu.make_async_copy(fac.at[0, i * cols:(i + 1) * cols], dst, fac_sem.at[i])
+        for i, dst in enumerate((fa_hbm, fb_hbm))
+    ]
     for i, (src, dst) in enumerate(((a_v, a_hbm), (b_v, b_hbm))):
         for k in range(parts):
             r = pl.ds(k * step, step)
@@ -223,7 +227,6 @@
     full = (n * rows, cols)
     vmem = pl.BlockSpec(memory_space=pltpu.VMEM)
     hbm = pl.BlockSpec(memory_space=pl.ANY)
-    gain = norm_gain.reshape(1, rows)
     space = pl.BlockSpec(memory_space=pltpu.HBM)
     rank = high_gate.shape[0]
     grant = 65472 * 2**10 - (4 * full[0] * cols + 8 * cols) // 2**10 * 2**10 - 24 * 2**10
@@ -232,7 +235,7 @@
         out_shape=(
             pltpu.VMEM(full, jnp.bfloat16),
             pltpu.VMEM(full, jnp.bfloat16),
-            jax.ShapeDtypeStruct((1, 2 * cols), jnp.float32),
+            pltpu.VMEM((1, 2 * cols), jnp.float32),
         ),
         in_specs=[space] * 7,
         out_specs=(vmem, vmem, vmem),
@@ -259,18 +262,18 @@
             collective_id=0, has_side_effects=True, vmem_limit_bytes=grant
         ),
         name="merge_gather",
-    )(weight_gate, weight_up, low_gate.T, low_up.T, high_gate, high_up, gain)
+    )(weight_gate, weight_up, low_gate.T, low_up.T, high_gate, high_up, norm_gain)
     parts = 8
-    ready_gate, ready_up = pl.pallas_call(
+    return pl.pallas_call(
         functools.partial(write_kernel, parts),
-        out_shape=(jax.ShapeDtypeStruct(full, jnp.bfloat16),) * 2,
-        in_specs=[vmem, vmem],
-        out_specs=(hbm, hbm),
-        scratch_shapes=[pltpu.SemaphoreType.DMA((2, parts))],
+        out_shape=(jax.ShapeDtypeStruct(full, jnp.bfloat16),) * 2
+        + (jax.ShapeDtypeStruct((cols,), jnp.float32),) * 2,
+        in_specs=[vmem, vmem, vmem],
+        out_specs=(hbm,) * 4,
+        scratch_shapes=[pltpu.SemaphoreType.DMA((2, parts)), pltpu.SemaphoreType.DMA((2,))],
         compiler_params=pltpu.CompilerParams(vmem_limit_bytes=2**20),
         name="write_out",
-    )(gate, up)
-    return ready_gate, ready_up, fac[0, :cols], fac[0, cols:]
+    )(gate, up, fac)
 
 
 def solution(mesh):

time: 123 us -> 121 us (0.984)
  local copies, waits for them, and re-layouts: 1.9 us -> 0 us
    reshape x1 -> x0, local copies, waits for them, and re-layouts: 1.25 us -> none  [paired(): gain = norm_gain.reshape(1, rows)]
where the time goes in v1:
time: 121 us
  Pallas kernels  120 us (99%)
    pallas_call x1, Pallas kernels, paired(): pl.pallas_call(functools.partial(gather_kernel, n, chunks, raw), out_shap...  112 us
    pallas_call x1, Pallas kernels, paired(): pl.pallas_call(functools.partial(write_kernel, parts), out_shape=(jax.Sha...  8.46 us

profile of v1, /device:TPU:0, one launch (start us, length us, event | category | flops | bytes accessed | tf_op | source)
XLA Modules:
  0.0 120.7 jit_solution(18209232424493249129)
XLA Ops:
  0.6 111.6 %merge_gather.1 = (bf16[2560,2432]{1,0:T(8,128)(2,1)S(1)}, bf16[2560,2432]{1,0:T(8,128)(2,1)S(1)}, f32[1,4864]{1,0:T(1,128)S(1)}) custom-call(bf16[320,2432]{1,0:T(8,128)(2,1)} %wg_hbm.1, bf16[320,2432]{1,0:T(8,128)(2,1)} %wu_hbm.1, bf16[32,320]{1,0:T(8,128)(2,1)} %bitcast.2, bf16[32,320]{1,0:T(8,128)(2,1)} %bitcast.3, bf16[32,2432]{1,0:T(8,128)(2,1)} %hg_hbm.1, ...), custom_call_target="tpu_custom_call" | custom-call | tf_op jit(solution)/shard_map/merge_gather/pallas_call | solution.py:233
  112.2 8.5 %write_out.1 = (bf16[2560,2432]{1,0:T(8,128)(2,1)}, bf16[2560,2432]{1,0:T(8,128)(2,1)}, f32[2432]{0:T(1024)}, f32[2432]{0:T(1024)}) custom-call(bf16[2560,2432]{1,0:T(8,128)(2,1)S(1)} %get-tuple-element.7.a_v, bf16[2560,2432]{1,0:T(8,128)(2,1)S(1)} %get-tuple-element.8.b_v, f32[1,4864]{1,0:T(1,128)S(1)} %get-tuple-element.9.fac), custom_call_target="tpu_custom_call" | custom-call | tf_op jit(solution)/shard_map/write_out/pallas_call | solution.py:267

commit v2 on v1

v2 whole, which is shorter than its diff:
```python
import functools
import math

import jax
import jax.numpy as jnp
from jax import lax
from jax.experimental import pallas as pl
from jax.experimental.pallas import tpu as pltpu
from jax.sharding import PartitionSpec as P

mix_rate = 2.0
AXIS = "shard"


def local(weight_gate, low_gate, high_gate, weight_up, low_up, high_up, norm_gain):
    latest_gate = weight_gate.astype(jnp.float32) + mix_rate * jnp.dot(
        low_gate, high_gate, preferred_element_type=jnp.float32
    )
    latest_up = weight_up.astype(jnp.float32) + mix_rate * jnp.dot(
        low_up, high_up, preferred_element_type=jnp.float32
    )
    latest_gained_gate = latest_gate * norm_gain[:, None]
    latest_gained_up = latest_up * norm_gain[:, None]
    total_gate, total_up = lax.psum(
        (
            jnp.sum(latest_gained_gate * latest_gained_gate, axis=0),
            jnp.sum(latest_gained_up * latest_gained_up, axis=0),
        ),
        AXIS,
    )
    factor_gate = jnp.sqrt(total_gate)
    factor_up = jnp.sqrt(total_up)
    narrow_gate = (latest_gained_gate / factor_gate).astype(jnp.bfloat16)
    narrow_up = (latest_gained_up / factor_up).astype(jnp.bfloat16)
    ready_gate = lax.all_gather(narrow_gate, AXIS, axis=0, tiled=True)
    ready_up = lax.all_gather(narrow_up, AXIS, axis=0, tiled=True)
    return (ready_gate, ready_up, factor_gate, factor_up)


late = 0


def place():
    me = lax.axis_index(AXIS)
    core = lax.rem(me, 2)
    x = lax.rem(me // 2, 2)
    y = me // 4
    to_x = me + 2 - 4 * x
    to_y = me + 4 - 8 * y
    return me, core, me + 1 - 2 * core, to_x, to_y, to_x + 4 - 8 * y, 1 - 2 * core


def pairs(start, *sizes):
    out = []
    for z in sizes:
        for _ in range(2):
            out.append((start, z))
            start += z
    return out


def gather_kernel(
    unit, solo, wg_hbm, wu_hbm, lg_hbm, lu_hbm, hg_hbm, hu_hbm, gain_hbm,
    out_g, out_u, fac,
    w_v, l_v, h_v, gain_v, low_v, g_v, col_v, part, mine, heard, rf_v,
    raw_v, far_l, far_g, far_low, far_col,
    in_sem, small_send, small_recv, send, recv,
):
    rows, cols = wg_hbm.shape
    me, core, sib, to_x, to_y, diag, flip = place()
    early = 4 * unit
    shared_up = rows - solo
    raws = [(0, s, z) for s, z in pairs(0, unit, unit)]
    bulk = [(0, s, z) for s, z in pairs(early, 3 * unit)]
    bulk += [(1, s, z) for s, z in (
        pairs(0, 2 * unit, unit) if solo else pairs(0, 3 * unit, unit, unit))]
    alone = [(1, s, z) for s, z in pairs(shared_up, unit, unit)] if solo else []
    block = (0, 0, early)
    every = raws + bulk
    order = {c: i for i, c in enumerate(every + alone + [block])}
    outs = (out_g, out_u)

    barrier = pltpu.get_barrier_semaphore()
    for d in (to_x, to_y, sib):
        pl.semaphore_signal(barrier, inc=1, device_id={AXIS: d})

    gain_load = pltpu.make_async_copy(gain_hbm, gain_v.at[0], in_sem.at[6])
    low_loads, high_loads, loads = (
        [
            pltpu.make_async_copy(src, dst.at[a], in_sem.at[3 * a + i])
            for a, src in enumerate(pair)
        ]
        for i, (pair, dst) in enumerate((
            ((lg_hbm, lu_hbm), l_v), ((hg_hbm, hu_hbm), h_v), ((wg_hbm, wu_hbm), w_v)
        ))
    )
    gain_load.start()
    for a in range(2):
        for c in (low_loads[a], high_loads[a], loads[a]):
            c.start()

    started = []

    def keep(c):
        started.append(c)
        c.start()

    def remote(src, dst, slot, chunk, target):
        i = order[chunk]
        return pltpu.make_async_remote_copy(
            src_ref=src, dst_ref=dst, send_sem=send.at[slot, i],
            recv_sem=recv.at[slot, i], device_id={AXIS: target})

    def small(src, dst, i, target):
        return pltpu.make_async_remote_copy(
            src_ref=src, dst_ref=dst, send_sem=small_send.at[i],
            recv_sem=small_recv.at[i], device_id={AXIS: target})

    def piece(chunk, owner):
        a, s, z = chunk
        return outs[a].at[pl.ds(pl.multiple_of(owner * rows + s, 16), z), :]

    def move(slot, chunk, owner, target):
        p = piece(chunk, owner)
        return remote(p, p, slot, chunk, target)

    def raw_move(slot, chunk, at, target):
        _, s, z = chunk
        src = wg_hbm.at[s:s + z, :] if slot < 2 else raw_v.at[at, s:s + z, :]
        return remote(src, raw_v.at[slot if slot < 2 else 2, s:s + z, :], slot, chunk, target)

    def send_raw(chunk, x_only=None):
        if x_only is not False:
            keep(raw_move(0, chunk, 0, to_x))
        if x_only is not True:
            keep(raw_move(1, chunk, 0, to_y))

    pl.semaphore_wait(barrier, 3)
    send_raw(raws[0])
    send_raw(raws[1])

    gain_load.wait()
    col_v[...] = jnp.broadcast_to(gain_v[...], (128, rows)).T
    step = 2 * unit
    for a in range(2):
        low_loads[a].wait()
        low_v[a] = (mix_rate * l_v[a].astype(jnp.float32)).T.astype(jnp.bfloat16)
        high_loads[a].wait()
        loads[a].wait()
        acc = jnp.zeros((8, cols), jnp.float32)
        for s in range(0, rows, step):
            r = pl.ds(s, step)
            prod = jnp.dot(low_v[a, r, :], h_v[a], preferred_element_type=jnp.float32)
            new = (w_v[a, r, :].astype(jnp.float32) + prod) * col_v[r, 0:1]
            g_v[a, r, :] = new
            acc = acc + jnp.sum((new * new).reshape(step // 8, 8, cols), axis=0)
        part[a] = jnp.sum(acc, axis=0, keepdims=True)

    keep(small(part.at[1 - core], heard.at[0], 0, sib))
    low_own, gain_own = l_v.at[0, :, :early], gain_v.at[:, :early]
    for i, d in enumerate((to_x, to_y)):
        keep(small(low_own, far_l.at[i], 4 + i, d))
        keep(small(gain_own, far_g.at[i], 7 + i, d))
    small(part.at[0], heard.at[0], 0, sib).wait_recv()
    mine[0] = part[core] + heard[0]
    send_raw(raws[2], False)
    keep(small(mine.at[0], heard.at[1], 1, to_x))
    send_raw(raws[2], True)
    small(mine.at[0], heard.at[1], 1, to_x).wait_recv()
    mine[1] = mine[0] + heard[1]
    send_raw(raws[3], True)
    keep(small(mine.at[1], heard.at[2], 2, to_y))
    send_raw(raws[3], False)
    small(mine.at[1], heard.at[2], 2, to_y).wait_recv()
    mine[2 + core] = mine[1] + heard[2]
    keep(small(mine.at[2 + core], mine.at[2 + core], 3, sib))
    small(mine.at[2], mine.at[2], 3, sib).wait_recv()
    for a in range(2):
        factor = jnp.sqrt(mine[2 + a])
        fac[a] = factor
        rf_v[a] = 1.0 / factor

    def scale(chunk):
        a, s, z = chunk
        r = pl.ds(pl.multiple_of(me * rows + s, 16), z)
        outs[a][r, :] = (g_v[a, s:s + z, :] * rf_v[a]).astype(jnp.bfloat16)

    def send_own(chunk):
        keep(move(0, chunk, me, to_x))
        keep(move(1, chunk, me, to_y))
        keep(move(2, chunk, me, sib))

    for i, chunk in enumerate(bulk):
        scale(chunk)
        if i:
            send_own(bulk[i - 1])
    scale(block)
    send_own(bulk[-1])
    for chunk in alone:
        scale(chunk)
    keep(move(2, block, me, sib))

    low_x, low_y = (small(low_own, far_l.at[i], 4 + i, to_x) for i in range(2))
    gain_x, gain_y = (small(gain_own, far_g.at[i], 7 + i, to_x) for i in range(2))
    low_x.wait_recv()
    keep(small(far_l.at[0], far_l.at[2], 6, to_y))
    gain_x.wait_recv()
    keep(small(far_g.at[0], far_g.at[2], 9, to_y))
    low_y.wait_recv()
    gain_y.wait_recv()

    def correct(i, owner):
        far_low[i] = (mix_rate * far_l[i].astype(jnp.float32)).T.astype(jnp.bfloat16)
        far_col[i] = jnp.broadcast_to(far_g[i], (128, early)).T
        for s in range(0, early, step):
            r = pl.ds(s, step)
            prod = jnp.dot(far_low[i, r, :], h_v[0], preferred_element_type=jnp.float32)
            new = (raw_v[i, r, :].astype(jnp.float32) + prod) * far_col[i, r, 0:1]
            o = pl.ds(pl.multiple_of(owner * rows + s, 16), step)
            out_g[o, :] = (new * rf_v[0]).astype(jnp.bfloat16)

    for i, chunk in enumerate(raws):
        raw_move(0, chunk, 0, to_x).wait_recv()
        if i % 2 == 0:
            keep(raw_move(5, chunk, 0, to_y))
        raw_move(1, chunk, 0, to_y).wait_recv()
        if i % 2 == 1:
            keep(raw_move(5, chunk, 1, to_x))
    correct(0, to_x)
    correct(1, to_y)

    def relay(i, chunk, keep, forward):
        move(0, chunk, to_x, to_x).wait_recv()
        if i % 2 == 0:
            keep(move(5, chunk, to_x, to_y))
        if forward:
            keep(move(3, chunk, to_x, sib))
        move(1, chunk, to_y, to_y).wait_recv()
        if i % 2 == 1:
            keep(move(5, chunk, to_y, to_x))
        if forward:
            keep(move(4, chunk, to_y, sib))

    for i, chunk in enumerate(bulk):
        relay(i, chunk, keep, True)
        if i == 0:
            keep(move(3, block, to_x, sib))
            keep(move(4, block, to_y, sib))

    if solo:
        @pl.when(core == late)
        def _():
            for chunk in alone:
                move(0, chunk, me, to_x).start()
                move(1, chunk, me, to_y).start()

    for chunk in raws:
        raw_move(5, chunk, 0, to_x).wait_recv()
    small(far_l.at[0], far_l.at[2], 6, to_y).wait_recv()
    small(far_g.at[0], far_g.at[2], 9, to_y).wait_recv()
    correct(2, diag)
    for i, chunk in enumerate(bulk):
        move(5, chunk, diag, to_x).wait_recv()
        keep(move(6, chunk, diag, sib))
        if i == 0:
            keep(move(6, block, diag, sib))
    for chunk in [block] + bulk:
        move(2, chunk, sib, sib).wait_recv()
        move(3, chunk, to_x + flip, sib).wait_recv()
        move(4, chunk, to_y + flip, sib).wait_recv()
        move(6, chunk, diag + flip, sib).wait_recv()

    if solo:
        @pl.when(core == late)
        def _():
            own = []

            def go(c):
                own.append(c)
                c.start()

            for i, chunk in enumerate(alone):
                relay(i, chunk, go, False)
            for chunk in alone:
                move(5, chunk, diag, to_x).wait_recv()
                move(0, chunk, me, to_x).wait_send()
                move(1, chunk, me, to_y).wait_send()
            for c in own:
                c.wait_send()

    for c in started:
        c.wait_send()


def tail_kernel(rows, unit, up, after, tail, ready, send, recv):
    solo = tail.shape[1]
    me, core, sib, to_x, to_y, diag, flip = place()
    chunks = pairs(0, unit, unit)
    whole = (0, solo)
    lines = len(chunks)
    barrier = pltpu.get_barrier_semaphore()

    def remote(src, dst, slot, i, target):
        return pltpu.make_async_remote_copy(
            src_ref=src, dst_ref=dst, send_sem=send.at[slot, i],
            recv_sem=recv.at[slot, i], device_id={AXIS: target})

    def held(owner, s, z):
        return up.at[pl.ds(pl.multiple_of(owner * rows + rows - solo + s, 16), z), :]

    def move(slot, i, chunk, owner, target, first=False):
        s, z = chunk
        dst = tail.at[owner, s:s + z, :]
        return remote(held(owner, s, z) if first else dst, dst, slot, i, target)

    def copy(owner):
        r = pl.ds(pl.multiple_of(owner * rows + rows - solo, 16), solo)
        tail[owner] = up[r, :]

    @pl.when(core != late)
    def _():
        started = []

        def keep(c):
            started.append(c)
            c.start()

        for d in (to_x, to_y, sib):
            pl.semaphore_signal(barrier, inc=1, device_id={AXIS: d})
        pl.semaphore_wait(barrier, 2)
        for i, c in enumerate(chunks):
            keep(move(0, i, c, me, to_x, True))
            keep(move(1, i, c, me, to_y, True))
        copy(me)
        for i, c in enumerate(chunks):
            move(0, i, c, to_x, to_x).wait_recv()
            if i % 2 == 0:
                keep(move(5, i, c, to_x, to_y))
            move(1, i, c, to_y, to_y).wait_recv()
            if i % 2 == 1:
                keep(move(5, i, c, to_y, to_x))
        pl.semaphore_wait(ready, 1)
        keep(move(2, 0, whole, me, sib, True))
        keep(move(3, 0, whole, to_x, sib))
        keep(move(4, 0, whole, to_y, sib))
        for i, c in enumerate(chunks):
            move(5, i, c, diag, to_x).wait_recv()
            keep(move(6, i, c, diag, sib))
        for i in range(4):
            move(7, i, whole, 2 * i + late, sib).wait_recv()
        for c in started:
            c.wait_send()

    @pl.when(core == late)
    def _():
        pl.semaphore_wait(barrier, 1)
        pl.semaphore_signal(ready, inc=1, device_id={AXIS: sib})
        out = [move(7, i, whole, 2 * i + late, sib, True) for i in range(4)]
        for c in out:
            c.start()
        for i in range(4):
            copy(2 * i + late)
        move(2, 0, whole, sib, sib).wait_recv()
        move(3, 0, whole, to_x + flip, sib).wait_recv()
        move(4, 0, whole, to_y + flip, sib).wait_recv()
        for i, c in enumerate(chunks):
            move(6, i, c, diag + flip, sib).wait_recv()
        for c in out:
            c.wait_send()


def write_kernel(rows, solo, a_v, b_v, fac, a_hbm, b_hbm, fa_hbm, fb_hbm, done, sem, fac_sem):
    done[...] = jnp.zeros_like(done)
    n = a_v.shape[0] // rows
    copies = [
        pltpu.make_async_copy(fac.at[i, 0], dst, fac_sem.at[i])
        for i, dst in enumerate((fa_hbm, fb_hbm))
    ]
    for i, (src, dst, z) in enumerate(((a_v, a_hbm, rows), (b_v, b_hbm, rows - solo))):
        for k in range(n):
            r = pl.ds(k * rows, z)
            copies.append(pltpu.make_async_copy(src.at[r, :], dst.at[r, :], sem.at[i, k]))
    for c in copies:
        c.start()
    for c in copies:
        c.wait()


def finish_kernel(rows, tail, before, b_hbm, sem):
    n, solo, _ = tail.shape
    copies = [
        pltpu.make_async_copy(
            tail.at[k], b_hbm.at[pl.ds((k + 1) * rows - solo, solo), :], sem.at[k])
        for k in range(n)
    ]
    for c in copies:
        c.start()
    for c in copies:
        c.wait()


def paired(n, weight_gate, low_gate, high_gate, weight_up, low_up, high_up, norm_gain):
    rows, cols = weight_gate.shape
    unit = rows // 10
    solo = 4 * unit
    early = 4 * unit
    full = (n * rows, cols)
    vmem = pl.BlockSpec(memory_space=pltpu.VMEM)
    hbm = pl.BlockSpec(memory_space=pl.ANY)
    space = pl.BlockSpec(memory_space=pltpu.HBM)
    rank = high_gate.shape[0]
    grant = 65472 * 2**10 - (4 * full[0] * cols + 8 * cols) // 2**10 * 2**10 - 24 * 2**10
    slots = 20
    gate, up, fac = pl.pallas_call(
        functools.partial(gather_kernel, unit, solo),
        out_shape=(
            pltpu.VMEM(full, jnp.bfloat16),
            pltpu.VMEM(full, jnp.bfloat16),
            pltpu.VMEM((2, 1, cols), jnp.float32),
        ),
        in_specs=[space] * 7,
        out_specs=(vmem, vmem, vmem),
        scratch_shapes=[
            pltpu.VMEM((2, rows, cols), jnp.bfloat16),
            pltpu.VMEM((2, rank, rows), jnp.bfloat16),
            pltpu.VMEM((2, rank, cols), jnp.bfloat16),
            pltpu.VMEM((1, rows), jnp.float32),
            pltpu.VMEM((2, rows, rank), jnp.bfloat16),
            pltpu.VMEM((2, rows, cols), jnp.float32),
            pltpu.VMEM((rows, 128), jnp.float32),
            pltpu.VMEM((2, 1, cols), jnp.float32),
            pltpu.VMEM((4, 1, cols), jnp.float32),
            pltpu.VMEM((3, 1, cols), jnp.float32),
            pltpu.VMEM((2, 1, cols), jnp.float32),
            pltpu.VMEM((3, early, cols), jnp.bfloat16),
            pltpu.VMEM((3, rank, early), jnp.bfloat16),
            pltpu.VMEM((3, 1, early), jnp.float32),
            pltpu.VMEM((3, early, rank), jnp.bfloat16),
            pltpu.VMEM((3, early, 128), jnp.float32),
            pltpu.SemaphoreType.DMA((7,)),
            pltpu.SemaphoreType.DMA((10,)),
            pltpu.SemaphoreType.DMA((10,)),
            pltpu.SemaphoreType.DMA((7, slots)),
            pltpu.SemaphoreType.DMA((7, slots)),
        ],
        compiler_params=pltpu.CompilerParams(
            collective_id=0, has_side_effects=True, vmem_limit_bytes=grant
        ),
        name="merge_gather",
    )(weight_gate, weight_up, low_gate.T, low_up.T, high_gate, high_up, norm_gain)
    whole = jax.ShapeDtypeStruct(full, jnp.bfloat16)
    ready_gate, ready_up, factor_gate, factor_up, done = pl.pallas_call(
        functools.partial(write_kernel, rows, solo),
        out_shape=(whole, whole) + (jax.ShapeDtypeStruct((cols,), jnp.float32),) * 2
        + (pltpu.VMEM((8, 128), jnp.float32),),
        in_specs=[vmem, vmem, vmem],
        out_specs=(hbm,) * 4 + (vmem,),
        scratch_shapes=[pltpu.SemaphoreType.DMA((2, n)), pltpu.SemaphoreType.DMA((2,))],
        compiler_params=pltpu.CompilerParams(vmem_limit_bytes=2**20),
        name="write_out",
    )(gate, up, fac)
    if solo:
        tail = pl.pallas_call(
            functools.partial(tail_kernel, rows, unit),
            out_shape=pltpu.VMEM((n, solo, cols), jnp.bfloat16),
            in_specs=[vmem, vmem],
            out_specs=vmem,
            scratch_shapes=[
                pltpu.SemaphoreType.REGULAR,
                pltpu.SemaphoreType.DMA((8, 4)),
                pltpu.SemaphoreType.DMA((8, 4)),
            ],
            compiler_params=pltpu.CompilerParams(
                collective_id=1, has_side_effects=True, vmem_limit_bytes=2**20
            ),
            name="tail_gather",
        )(up, done)
        ready_up = pl.pallas_call(
            functools.partial(finish_kernel, rows),
            out_shape=whole,
            in_specs=[vmem, hbm],
            out_specs=hbm,
            input_output_aliases={1: 0},
            scratch_shapes=[pltpu.SemaphoreType.DMA((n,))],
            compiler_params=pltpu.CompilerParams(vmem_limit_bytes=2**20),
            name="finish",
        )(tail, ready_up)
    return ready_gate, ready_up, factor_gate, factor_up


def solution(mesh):
    in_specs = (
        P("shard", "tp"),
        P("shard", None),
        P(None, "tp"),
        P("shard", "tp"),
        P("shard", None),
        P(None, "tp"),
        P("shard"),
    )
    out_specs = (P(None, "tp"), P(None, "tp"), P("tp"), P("tp"))
    n = mesh.shape[AXIS]
    side = math.isqrt(n // 2)
    body = functools.partial(paired, n) if side == 2 and 2 * side * side == n else local
    return jax.shard_map(body, mesh=mesh, in_specs=in_specs, out_specs=out_specs, check_vma=False)
```

time: 121 us -> 116 us (0.959)
  Pallas kernels: 120 us -> 115 us
    pallas_call x2 -> x4, Pallas kernels: 120 us -> 115 us  [the longest x1 100 us: paired(): pl.pallas_call(functools.partial(gather_kernel, unit, solo), out_shape=(p...]
where the time goes in v2:
time: 116 us; the launch traced here: 115 us
  Pallas kernels  115 us (99%)
    pallas_call x1, Pallas kernels, paired(): pl.pallas_call(functools.partial(gather_kernel, unit, solo), out_shape=(p...  100 us
    pallas_call x1, Pallas kernels, paired(): pl.pallas_call(functools.partial(write_kernel, rows, solo), out_shape=(wh...  6.94 us
    pallas_call x1, Pallas kernels, paired(): pl.pallas_call(functools.partial(tail_kernel, rows, unit), out_shape=pltp...  5.37 us
    pallas_call x1, Pallas kernels, paired(): pl.pallas_call(functools.partial(finish_kernel, rows), out_shape=whole, i...  2.33 us

profile of v2, /device:TPU:0, one launch (start us, length us, event | category | flops | bytes accessed | tf_op | source)
XLA Modules:
  0.0 115.4 jit_solution(362009524408214147)
XLA Ops:
  0.6 100.1 %merge_gather.1 = (bf16[2560,2432]{1,0:T(8,128)(2,1)S(1)}, bf16[2560,2432]{1,0:T(8,128)(2,1)S(1)}, f32[2,1,2432]{2,1,0:T(1,128)S(1)}) custom-call(bf16[320,2432]{1,0:T(8,128)(2,1)} %wg_hbm.1, bf16[320,2432]{1,0:T(8,128)(2,1)} %wu_hbm.1, bf16[32,320]{1,0:T(8,128)(2,1)} %bitcast.2, bf16[32,320]{1,0:T(8,128)(2,1)} %bitcast.3, bf16[32,2432]{1,0:T(8,128)(2,1)} %hg_hbm.1, ...), custom_call_target="tpu_custom_call" | custom-call | tf_op jit(solution)/shard_map/merge_gather/pallas_call | solution.py:414
  100.8 6.9 %write_out.1 = (bf16[2560,2432]{1,0:T(8,128)(2,1)}, bf16[2560,2432]{1,0:T(8,128)(2,1)}, f32[2432]{0:T(1024)}, f32[2432]{0:T(1024)}, f32[8,128]{1,0:T(8,128)S(1)}) custom-call(bf16[2560,2432]{1,0:T(8,128)(2,1)S(1)} %get-tuple-element.12.a_v, bf16[2560,2432]{1,0:T(8,128)(2,1)S(1)} %get-tuple-element.13.b_v.up, f32[2,1,2432]{2,1,0:T(1,128)S(1)} %get-tuple-element.14.fac), custom_call_target="tpu_custom_call" | custom-call | tf_op jit(solution)/shard_map/write_out/pallas_call | solution.py:452
  107.7 5.4 %tail_gather.1.tail = bf16[8,128,2432]{2,1,0:T(8,128)(2,1)S(1)} custom-call(bf16[2560,2432]{1,0:T(8,128)(2,1)S(1)} %get-tuple-element.13.b_v.up, f32[8,128]{1,0:T(8,128)S(1)} %get-tuple-element.16.after), custom_call_target="tpu_custom_call" | custom-call | tf_op jit(solution)/shard_map/tail_gather/pallas_call | solution.py:463
  113.1 2.3 %finish.1 = bf16[2560,2432]{1,0:T(8,128)(2,1)} custom-call(bf16[8,128,2432]{2,1,0:T(8,128)(2,1)S(1)} %tail_gather.1.tail, bf16[2560,2432]{1,0:T(8,128)(2,1)} %get-tuple-element.17.before), custom_call_target="tpu_custom_call", output_to_operand_aliasing={{}: (1, {})} | custom-call | tf_op jit(solution)/shard_map/finish/pallas_call | solution.py:478

commit v3 on v2

--- a/solution.py
+++ b/solution.py
@@ -38,6 +38,10 @@
 
 
 late = 0
+RAW = (4, 4)
+GATE = (12,)
+UP = (4, 4)
+ALONE = (8, 4)
 
 
 def place():
@@ -50,12 +54,12 @@
     return me, core, me + 1 - 2 * core, to_x, to_y, to_x + 4 - 8 * y, 1 - 2 * core
 
 
-def pairs(start, *sizes):
+def pairs(start, unit, sizes):
     out = []
     for z in sizes:
         for _ in range(2):
-            out.append((start, z))
-            start += z
+            out.append((start, z * unit))
+            start += z * unit
     return out
 
 
@@ -68,16 +72,16 @@
 ):
     rows, cols = wg_hbm.shape
     me, core, sib, to_x, to_y, diag, flip = place()
-    early = 4 * unit
+    early = 2 * sum(RAW) * unit
     shared_up = rows - solo
-    raws = [(0, s, z) for s, z in pairs(0, unit, unit)]
-    bulk = [(0, s, z) for s, z in pairs(early, 3 * unit)]
-    bulk += [(1, s, z) for s, z in (
-        pairs(0, 2 * unit, unit) if solo else pairs(0, 3 * unit, unit, unit))]
-    alone = [(1, s, z) for s, z in pairs(shared_up, unit, unit)] if solo else []
+    raws = [(0, s, z) for s, z in pairs(0, unit, RAW)]
+    bulk = [(0, s, z) for s, z in pairs(early, unit, GATE)]
+    bulk += [(1, s, z) for s, z in pairs(0, unit, UP)]
+    alone = [(1, s, z) for s, z in pairs(shared_up, unit, ALONE)]
+    own_tail = (1, shared_up, solo)
     block = (0, 0, early)
     every = raws + bulk
-    order = {c: i for i, c in enumerate(every + alone + [block])}
+    order = {c: i for i, c in enumerate(every + alone + [block, own_tail])}
     outs = (out_g, out_u)
 
     barrier = pltpu.get_barrier_semaphore()
@@ -118,7 +122,7 @@
 
     def piece(chunk, owner):
         a, s, z = chunk
-        return outs[a].at[pl.ds(pl.multiple_of(owner * rows + s, 16), z), :]
+        return outs[a].at[pl.ds(pl.multiple_of(owner * rows + s, 8), z), :]
 
     def move(slot, chunk, owner, target):
         p = piece(chunk, owner)
@@ -141,7 +145,7 @@
 
     gain_load.wait()
     col_v[...] = jnp.broadcast_to(gain_v[...], (128, rows)).T
-    step = 2 * unit
+    step = rows // 5
     for a in range(2):
         low_loads[a].wait()
         low_v[a] = (mix_rate * l_v[a].astype(jnp.float32)).T.astype(jnp.bfloat16)
@@ -182,7 +186,7 @@
 
     def scale(chunk):
         a, s, z = chunk
-        r = pl.ds(pl.multiple_of(me * rows + s, 16), z)
+        r = pl.ds(pl.multiple_of(me * rows + s, 8), z)
         outs[a][r, :] = (g_v[a, s:s + z, :] * rf_v[a]).astype(jnp.bfloat16)
 
     def send_own(chunk):
@@ -199,6 +203,7 @@
     for chunk in alone:
         scale(chunk)
     keep(move(2, block, me, sib))
+    keep(move(2, own_tail, me, sib))
 
     low_x, low_y = (small(low_own, far_l.at[i], 4 + i, to_x) for i in range(2))
     gain_x, gain_y = (small(gain_own, far_g.at[i], 7 + i, to_x) for i in range(2))
@@ -212,11 +217,11 @@
     def correct(i, owner):
         far_low[i] = (mix_rate * far_l[i].astype(jnp.float32)).T.astype(jnp.bfloat16)
         far_col[i] = jnp.broadcast_to(far_g[i], (128, early)).T
-        for s in range(0, early, step):
-            r = pl.ds(s, step)
+        for s in range(0, early, early // 2):
+            r = pl.ds(s, early // 2)
             prod = jnp.dot(far_low[i, r, :], h_v[0], preferred_element_type=jnp.float32)
             new = (raw_v[i, r, :].astype(jnp.float32) + prod) * far_col[i, r, 0:1]
-            o = pl.ds(pl.multiple_of(owner * rows + s, 16), step)
+            o = pl.ds(pl.multiple_of(owner * rows + s, 8), early // 2)
             out_g[o, :] = (new * rf_v[0]).astype(jnp.bfloat16)
 
     for i, chunk in enumerate(raws):
@@ -247,12 +252,11 @@
             keep(move(3, block, to_x, sib))
             keep(move(4, block, to_y, sib))
 
-    if solo:
-        @pl.when(core == late)
-        def _():
-            for chunk in alone:
-                move(0, chunk, me, to_x).start()
-                move(1, chunk, me, to_y).start()
+    @pl.when(core == late)
+    def _():
+        for chunk in alone:
+            move(0, chunk, me, to_x).start()
+            move(1, chunk, me, to_y).start()
 
     for chunk in raws:
         raw_move(5, chunk, 0, to_x).wait_recv()
@@ -269,24 +273,24 @@
         move(3, chunk, to_x + flip, sib).wait_recv()
         move(4, chunk, to_y + flip, sib).wait_recv()
         move(6, chunk, diag + flip, sib).wait_recv()
-
-    if solo:
-        @pl.when(core == late)
-        def _():
-            own = []
-
-            def go(c):
-                own.append(c)
-                c.start()
-
-            for i, chunk in enumerate(alone):
-                relay(i, chunk, go, False)
-            for chunk in alone:
-                move(5, chunk, diag, to_x).wait_recv()
-                move(0, chunk, me, to_x).wait_send()
-                move(1, chunk, me, to_y).wait_send()
-            for c in own:
-                c.wait_send()
+    move(2, own_tail, sib, sib).wait_recv()
+
+    @pl.when(core == late)
+    def _():
+        own = []
+
+        def go(c):
+            own.append(c)
+            c.start()
+
+        for i, chunk in enumerate(alone):
+            relay(i, chunk, go, False)
+        for chunk in alone:
+            move(5, chunk, diag, to_x).wait_recv()
+            move(0, chunk, me, to_x).wait_send()
+            move(1, chunk, me, to_y).wait_send()
+        for c in own:
+            c.wait_send()
 
     for c in started:
         c.wait_send()
@@ -295,9 +299,9 @@
 def tail_kernel(rows, unit, up, after, tail, ready, send, recv):
     solo = tail.shape[1]
     me, core, sib, to_x, to_y, diag, flip = place()
-    chunks = pairs(0, unit, unit)
+    chunks = pairs(0, unit, ALONE)
     whole = (0, solo)
-    lines = len(chunks)
+    rest = (to_x, to_y, diag)
     barrier = pltpu.get_barrier_semaphore()
 
     def remote(src, dst, slot, i, target):
@@ -306,7 +310,7 @@
             recv_sem=recv.at[slot, i], device_id={AXIS: target})
 
     def held(owner, s, z):
-        return up.at[pl.ds(pl.multiple_of(owner * rows + rows - solo + s, 16), z), :]
+        return up.at[pl.ds(pl.multiple_of(owner * rows + rows - solo + s, 8), z), :]
 
     def move(slot, i, chunk, owner, target, first=False):
         s, z = chunk
@@ -314,7 +318,7 @@
         return remote(held(owner, s, z) if first else dst, dst, slot, i, target)
 
     def copy(owner):
-        r = pl.ds(pl.multiple_of(owner * rows + rows - solo, 16), solo)
+        r = pl.ds(pl.multiple_of(owner * rows + rows - solo, 8), solo)
         tail[owner] = up[r, :]
 
     @pl.when(core != late)
@@ -331,7 +335,6 @@
         for i, c in enumerate(chunks):
             keep(move(0, i, c, me, to_x, True))
             keep(move(1, i, c, me, to_y, True))
-        copy(me)
         for i, c in enumerate(chunks):
             move(0, i, c, to_x, to_x).wait_recv()
             if i % 2 == 0:
@@ -340,14 +343,13 @@
             if i % 2 == 1:
                 keep(move(5, i, c, to_y, to_x))
         pl.semaphore_wait(ready, 1)
-        keep(move(2, 0, whole, me, sib, True))
         keep(move(3, 0, whole, to_x, sib))
         keep(move(4, 0, whole, to_y, sib))
         for i, c in enumerate(chunks):
             move(5, i, c, diag, to_x).wait_recv()
             keep(move(6, i, c, diag, sib))
-        for i in range(4):
-            move(7, i, whole, 2 * i + late, sib).wait_recv()
+        for i, owner in enumerate(rest):
+            move(7, i, whole, owner + flip, sib).wait_recv()
         for c in started:
             c.wait_send()
 
@@ -355,12 +357,11 @@
     def _():
         pl.semaphore_wait(barrier, 1)
         pl.semaphore_signal(ready, inc=1, device_id={AXIS: sib})
-        out = [move(7, i, whole, 2 * i + late, sib, True) for i in range(4)]
+        out = [move(7, i, whole, owner, sib, True) for i, owner in enumerate(rest)]
         for c in out:
             c.start()
-        for i in range(4):
-            copy(2 * i + late)
-        move(2, 0, whole, sib, sib).wait_recv()
+        for owner in rest:
+            copy(owner)
         move(3, 0, whole, to_x + flip, sib).wait_recv()
         move(4, 0, whole, to_y + flip, sib).wait_recv()
         for i, c in enumerate(chunks):
@@ -372,13 +373,16 @@
 def write_kernel(rows, solo, a_v, b_v, fac, a_hbm, b_hbm, fa_hbm, fb_hbm, done, sem, fac_sem):
     done[...] = jnp.zeros_like(done)
     n = a_v.shape[0] // rows
+    first = lax.axis_index(AXIS) // 2 * 2
     copies = [
         pltpu.make_async_copy(fac.at[i, 0], dst, fac_sem.at[i])
         for i, dst in enumerate((fa_hbm, fb_hbm))
     ]
-    for i, (src, dst, z) in enumerate(((a_v, a_hbm, rows), (b_v, b_hbm, rows - solo))):
-        for k in range(n):
-            r = pl.ds(k * rows, z)
+    for k in range(n):
+        for i, (src, dst) in enumerate(((a_v, a_hbm), (b_v, b_hbm))):
+            owner = lax.rem(first + k, n)
+            z = rows - solo if i and k > 1 else rows
+            r = pl.ds(pl.multiple_of(owner * rows, 8), z)
             copies.append(pltpu.make_async_copy(src.at[r, :], dst.at[r, :], sem.at[i, k]))
     for c in copies:
         c.start()
@@ -388,11 +392,12 @@
 
 def finish_kernel(rows, tail, before, b_hbm, sem):
     n, solo, _ = tail.shape
-    copies = [
-        pltpu.make_async_copy(
-            tail.at[k], b_hbm.at[pl.ds((k + 1) * rows - solo, solo), :], sem.at[k])
-        for k in range(n)
-    ]
+    first = lax.axis_index(AXIS) // 2 * 2
+    copies = []
+    for k in range(2, n):
+        owner = lax.rem(first + k, n)
+        r = pl.ds(pl.multiple_of((owner + 1) * rows - solo, 8), solo)
+        copies.append(pltpu.make_async_copy(tail.at[owner], b_hbm.at[r, :], sem.at[k]))
     for c in copies:
         c.start()
     for c in copies:
@@ -401,9 +406,9 @@
 
 def paired(n, weight_gate, low_gate, high_gate, weight_up, low_up, high_up, norm_gain):
     rows, cols = weight_gate.shape
-    unit = rows // 10
-    solo = 4 * unit
-    early = 4 * unit
+    unit = rows // 40
+    solo = 2 * sum(ALONE) * unit
+    early = 2 * sum(RAW) * unit
     full = (n * rows, cols)
     vmem = pl.BlockSpec(memory_space=pltpu.VMEM)
     hbm = pl.BlockSpec(memory_space=pl.ANY)
@@ -459,32 +464,31 @@
         compiler_params=pltpu.CompilerParams(vmem_limit_bytes=2**20),
         name="write_out",
     )(gate, up, fac)
-    if solo:
-        tail = pl.pallas_call(
-            functools.partial(tail_kernel, rows, unit),
-            out_shape=pltpu.VMEM((n, solo, cols), jnp.bfloat16),
-            in_specs=[vmem, vmem],
-            out_specs=vmem,
-            scratch_shapes=[
-                pltpu.SemaphoreType.REGULAR,
-                pltpu.SemaphoreType.DMA((8, 4)),
-                pltpu.SemaphoreType.DMA((8, 4)),
-            ],
-            compiler_params=pltpu.CompilerParams(
-                collective_id=1, has_side_effects=True, vmem_limit_bytes=2**20
-            ),
-            name="tail_gather",
-        )(up, done)
-        ready_up = pl.pallas_call(
-            functools.partial(finish_kernel, rows),
-            out_shape=whole,
-            in_specs=[vmem, hbm],
-            out_specs=hbm,
-            input_output_aliases={1: 0},
-            scratch_shapes=[pltpu.SemaphoreType.DMA((n,))],
-            compiler_params=pltpu.CompilerParams(vmem_limit_bytes=2**20),
-            name="finish",
-        )(tail, ready_up)
+    tail = pl.pallas_call(
+        functools.partial(tail_kernel, rows, unit),
+        out_shape=pltpu.VMEM((n, solo, cols), jnp.bfloat16),
+        in_specs=[vmem, vmem],
+        out_specs=vmem,
+        scratch_shapes=[
+            pltpu.SemaphoreType.REGULAR,
+            pltpu.SemaphoreType.DMA((8, 2 * len(ALONE))),
+            pltpu.SemaphoreType.DMA((8, 2 * len(ALONE))),
+        ],
+        compiler_params=pltpu.CompilerParams(
+            collective_id=1, has_side_effects=True, vmem_limit_bytes=2**20
+        ),
+        name="tail_gather",
+    )(up, done)
+    ready_up = pl.pallas_call(
+        functools.partial(finish_kernel, rows),
+        out_shape=whole,
+        in_specs=[vmem, hbm],
+        out_specs=hbm,
+        input_output_aliases={1: 0},
+        scratch_shapes=[pltpu.SemaphoreType.DMA((n,))],
+        compiler_params=pltpu.CompilerParams(vmem_limit_bytes=2**20),
+        name="finish",
+    )(tail, ready_up)
     return ready_gate, ready_up, factor_gate, factor_up
 
 

time: 116 us -> 111 us (0.957)
  Pallas kernels: 115 us -> 110 us
    pallas_call x1, Pallas kernels: 100 us -> 94.8 us  [paired(): pl.pallas_call(functools.partial(gather_kernel, unit, solo), out_shape=(p...]
where the time goes in v3:
time: 111 us
  Pallas kernels  110 us (99%)
    pallas_call x1, Pallas kernels, paired(): pl.pallas_call(functools.partial(gather_kernel, unit, solo), out_shape=(p...  94.8 us
    pallas_call x1, Pallas kernels, paired(): pl.pallas_call(functools.partial(write_kernel, rows, solo), out_shape=(wh...  6.76 us
    pallas_call x1, Pallas kernels, paired(): pl.pallas_call(functools.partial(tail_kernel, rows, unit), out_shape=pltp...  5.86 us
    pallas_call x1, Pallas kernels, paired(): pl.pallas_call(functools.partial(finish_kernel, rows), out_shape=whole, i...  2.56 us

profile of v3, /device:TPU:0, one launch (start us, length us, event | category | flops | bytes accessed | tf_op | source)
XLA Modules:
  0.0 110.6 jit_solution(5567405459723661752)
XLA Ops:
  0.6 94.8 %merge_gather.1 = (bf16[2560,2432]{1,0:T(8,128)(2,1)S(1)}, bf16[2560,2432]{1,0:T(8,128)(2,1)S(1)}, f32[2,1,2432]{2,1,0:T(1,128)S(1)}) custom-call(bf16[320,2432]{1,0:T(8,128)(2,1)} %wg_hbm.1, bf16[320,2432]{1,0:T(8,128)(2,1)} %wu_hbm.1, bf16[32,320]{1,0:T(8,128)(2,1)} %bitcast.2, bf16[32,320]{1,0:T(8,128)(2,1)} %bitcast.3, bf16[32,2432]{1,0:T(8,128)(2,1)} %hg_hbm.1, ...), custom_call_target="tpu_custom_call" | custom-call | tf_op jit(solution)/shard_map/merge_gather/pallas_call | solution.py:419
  95.4 6.8 %write_out.1 = (bf16[2560,2432]{1,0:T(8,128)(2,1)}, bf16[2560,2432]{1,0:T(8,128)(2,1)}, f32[2432]{0:T(1024)}, f32[2432]{0:T(1024)}, f32[8,128]{1,0:T(8,128)S(1)}) custom-call(bf16[2560,2432]{1,0:T(8,128)(2,1)S(1)} %get-tuple-element.12.a_v, bf16[2560,2432]{1,0:T(8,128)(2,1)S(1)} %get-tuple-element.13.b_v.up, f32[2,1,2432]{2,1,0:T(1,128)S(1)} %get-tuple-element.14.fac), custom_call_target="tpu_custom_call" | custom-call | tf_op jit(solution)/shard_map/write_out/pallas_call | solution.py:457
  102.2 5.9 %tail_gather.1.tail = bf16[8,192,2432]{2,1,0:T(8,128)(2,1)S(1)} custom-call(bf16[2560,2432]{1,0:T(8,128)(2,1)S(1)} %get-tuple-element.13.b_v.up, f32[8,128]{1,0:T(8,128)S(1)} %get-tuple-element.16.after), custom_call_target="tpu_custom_call" | custom-call | tf_op jit(solution)/shard_map/tail_gather/pallas_call | solution.py:467
  108.1 2.6 %finish.1 = bf16[2560,2432]{1,0:T(8,128)(2,1)} custom-call(bf16[8,192,2432]{2,1,0:T(8,128)(2,1)S(1)} %tail_gather.1.tail, bf16[2560,2432]{1,0:T(8,128)(2,1)} %get-tuple-element.17.before), custom_call_target="tpu_custom_call", output_to_operand_aliasing={{}: (1, {})} | custom-call | tf_op jit(solution)/shard_map/finish/pallas_call | solution.py:482

commit v4 on v3

--- a/solution.py
+++ b/solution.py
@@ -89,19 +89,25 @@
         pl.semaphore_signal(barrier, inc=1, device_id={AXIS: d})
 
     gain_load = pltpu.make_async_copy(gain_hbm, gain_v.at[0], in_sem.at[6])
-    low_loads, high_loads, loads = (
+    low_loads, high_loads = (
         [
             pltpu.make_async_copy(src, dst.at[a], in_sem.at[3 * a + i])
             for a, src in enumerate(pair)
         ]
-        for i, (pair, dst) in enumerate((
-            ((lg_hbm, lu_hbm), l_v), ((hg_hbm, hu_hbm), h_v), ((wg_hbm, wu_hbm), w_v)
-        ))
+        for i, (pair, dst) in enumerate((((lg_hbm, lu_hbm), l_v), ((hg_hbm, hu_hbm), h_v)))
     )
-    gain_load.start()
-    for a in range(2):
-        for c in (low_loads[a], high_loads[a], loads[a]):
-            c.start()
+    loads = [
+        pltpu.make_async_copy(wg_hbm.at[early:, :], w_v.at[0, early:, :], in_sem.at[2]),
+        pltpu.make_async_copy(wu_hbm, w_v.at[1], in_sem.at[5]),
+    ]
+    raw_loads = [
+        pltpu.make_async_copy(wg_hbm.at[s:s + z, :], w_v.at[0, s:s + z, :], in_sem.at[7 + i])
+        for i, (_, s, z) in enumerate(raws)
+    ]
+    for c in raw_loads[:2] + [low_loads[0], gain_load, high_loads[0]] + raw_loads[2:]:
+        c.start()
+    for c in (loads[0], low_loads[1], high_loads[1], loads[1]):
+        c.start()
 
     started = []
 
@@ -130,24 +136,29 @@
 
     def raw_move(slot, chunk, at, target):
         _, s, z = chunk
-        src = wg_hbm.at[s:s + z, :] if slot < 2 else raw_v.at[at, s:s + z, :]
+        src = w_v.at[0, s:s + z, :] if slot < 2 else raw_v.at[at, s:s + z, :]
         return remote(src, raw_v.at[slot if slot < 2 else 2, s:s + z, :], slot, chunk, target)
 
-    def send_raw(chunk, x_only=None):
-        if x_only is not False:
-            keep(raw_move(0, chunk, 0, to_x))
-        if x_only is not True:
-            keep(raw_move(1, chunk, 0, to_y))
-
     pl.semaphore_wait(barrier, 3)
-    send_raw(raws[0])
-    send_raw(raws[1])
-
+    for c, chunk in list(zip(raw_loads, raws))[:2]:
+        c.wait()
+        keep(raw_move(0, chunk, 0, to_x))
+        keep(raw_move(1, chunk, 0, to_y))
+    low_own, gain_own = l_v.at[0, :, :early], gain_v.at[:, :early]
+    low_loads[0].wait()
     gain_load.wait()
+    for i, d in enumerate((to_x, to_y)):
+        keep(small(low_own, far_l.at[i], 4 + i, d))
+        keep(small(gain_own, far_g.at[i], 7 + i, d))
+
     col_v[...] = jnp.broadcast_to(gain_v[...], (128, rows)).T
     step = rows // 5
     for a in range(2):
-        low_loads[a].wait()
+        if a:
+            low_loads[a].wait()
+        else:
+            for c in raw_loads[2:]:
+                c.wait()
         low_v[a] = (mix_rate * l_v[a].astype(jnp.float32)).T.astype(jnp.bfloat16)
         high_loads[a].wait()
         loads[a].wait()
@@ -160,27 +171,40 @@
             acc = acc + jnp.sum((new * new).reshape(step // 8, 8, cols), axis=0)
         part[a] = jnp.sum(acc, axis=0, keepdims=True)
 
-    keep(small(part.at[1 - core], heard.at[0], 0, sib))
-    low_own, gain_own = l_v.at[0, :, :early], gain_v.at[:, :early]
-    for i, d in enumerate((to_x, to_y)):
-        keep(small(low_own, far_l.at[i], 4 + i, d))
-        keep(small(gain_own, far_g.at[i], 7 + i, d))
-    small(part.at[0], heard.at[0], 0, sib).wait_recv()
-    mine[0] = part[core] + heard[0]
-    send_raw(raws[2], False)
-    keep(small(mine.at[0], heard.at[1], 1, to_x))
-    send_raw(raws[2], True)
-    small(mine.at[0], heard.at[1], 1, to_x).wait_recv()
-    mine[1] = mine[0] + heard[1]
-    send_raw(raws[3], True)
-    keep(small(mine.at[1], heard.at[2], 2, to_y))
-    send_raw(raws[3], False)
-    small(mine.at[1], heard.at[2], 2, to_y).wait_recv()
-    mine[2 + core] = mine[1] + heard[2]
-    keep(small(mine.at[2 + core], mine.at[2 + core], 3, sib))
-    small(mine.at[2], mine.at[2], 3, sib).wait_recv()
+    sum_pair = small(part, heard.at[0], 0, sib)
+    sum_x = small(mine.at[0], heard.at[1], 1, to_x)
+    sum_y = small(mine.at[1], heard.at[2], 2, to_y)
+    sum_all = small(mine.at[2], mine.at[2], 3, sib)
+
+    @pl.when(core == late)
+    def _():
+        sum_pair.start()
+        for chunk in raws[2:]:
+            raw_move(0, chunk, 0, to_x).start()
+            raw_move(1, chunk, 0, to_y).start()
+        sum_all.wait_recv()
+
+    @pl.when(core != late)
+    def _():
+        sum_pair.wait_recv()
+        mine[0] = part[...] + heard[0]
+        raw_move(1, raws[2], 0, to_y).start()
+        sum_x.start()
+        raw_move(0, raws[2], 0, to_x).start()
+        sum_x.wait_recv()
+        mine[1] = mine[0] + heard[1]
+        raw_move(0, raws[3], 0, to_x).start()
+        sum_y.start()
+        raw_move(1, raws[3], 0, to_y).start()
+        sum_y.wait_recv()
+        mine[2] = mine[1] + heard[2]
+        sum_all.start()
+
+    for chunk in raws[2:]:
+        started.append(raw_move(0, chunk, 0, to_x))
+        started.append(raw_move(1, chunk, 0, to_y))
     for a in range(2):
-        factor = jnp.sqrt(mine[2 + a])
+        factor = jnp.sqrt(mine[2, a])
         fac[a] = factor
         rf_v[a] = 1.0 / factor
 
@@ -289,7 +313,12 @@
             move(5, chunk, diag, to_x).wait_recv()
             move(0, chunk, me, to_x).wait_send()
             move(1, chunk, me, to_y).wait_send()
-        for c in own:
+        for c in own + [sum_pair]:
+            c.wait_send()
+
+    @pl.when(core != late)
+    def _():
+        for c in (sum_x, sum_y, sum_all):
             c.wait_send()
 
     for c in started:
@@ -434,15 +463,15 @@
             pltpu.VMEM((2, rows, cols), jnp.float32),
             pltpu.VMEM((rows, 128), jnp.float32),
             pltpu.VMEM((2, 1, cols), jnp.float32),
-            pltpu.VMEM((4, 1, cols), jnp.float32),
-            pltpu.VMEM((3, 1, cols), jnp.float32),
+            pltpu.VMEM((3, 2, 1, cols), jnp.float32),
+            pltpu.VMEM((3, 2, 1, cols), jnp.float32),
             pltpu.VMEM((2, 1, cols), jnp.float32),
             pltpu.VMEM((3, early, cols), jnp.bfloat16),
             pltpu.VMEM((3, rank, early), jnp.bfloat16),
             pltpu.VMEM((3, 1, early), jnp.float32),
             pltpu.VMEM((3, early, rank), jnp.bfloat16),
             pltpu.VMEM((3, early, 128), jnp.float32),
-            pltpu.SemaphoreType.DMA((7,)),
+            pltpu.SemaphoreType.DMA((7 + 2 * len(RAW),)),
             pltpu.SemaphoreType.DMA((10,)),
             pltpu.SemaphoreType.DMA((10,)),
             pltpu.SemaphoreType.DMA((7, slots)),

time: 111 us -> 110 us (level)
  no operation moved by 1% of the time
where the time goes in v4:
time: 110 us
  Pallas kernels  110 us (100%)
    pallas_call x1, Pallas kernels, paired(): pl.pallas_call(functools.partial(gather_kernel, unit, solo), out_shape=(p...  94.6 us
    pallas_call x1, Pallas kernels, paired(): pl.pallas_call(functools.partial(write_kernel, rows, solo), out_shape=(wh...  6.76 us
    pallas_call x1, Pallas kernels, paired(): pl.pallas_call(functools.partial(tail_kernel, rows, unit), out_shape=pltp...  5.81 us
    pallas_call x1, Pallas kernels, paired(): pl.pallas_call(functools.partial(finish_kernel, rows), out_shape=whole, i...  2.56 us

profile of v4, /device:TPU:0, one launch (start us, length us, event | category | flops | bytes accessed | tf_op | source)
XLA Modules:
  0.0 110.3 jit_solution(10908300546134448702)
XLA Ops:
  0.6 94.6 %merge_gather.1 = (bf16[2560,2432]{1,0:T(8,128)(2,1)S(1)}, bf16[2560,2432]{1,0:T(8,128)(2,1)S(1)}, f32[2,1,2432]{2,1,0:T(1,128)S(1)}) custom-call(bf16[320,2432]{1,0:T(8,128)(2,1)} %wg_hbm.1, bf16[320,2432]{1,0:T(8,128)(2,1)} %wu_hbm.1, bf16[32,320]{1,0:T(8,128)(2,1)} %bitcast.2, bf16[32,320]{1,0:T(8,128)(2,1)} %bitcast.3, bf16[32,2432]{1,0:T(8,128)(2,1)} %hg_hbm.1, ...), custom_call_target="tpu_custom_call" | custom-call | tf_op jit(solution)/shard_map/merge_gather/pallas_call | solution.py:448
  95.2 6.8 %write_out.1 = (bf16[2560,2432]{1,0:T(8,128)(2,1)}, bf16[2560,2432]{1,0:T(8,128)(2,1)}, f32[2432]{0:T(1024)}, f32[2432]{0:T(1024)}, f32[8,128]{1,0:T(8,128)S(1)}) custom-call(bf16[2560,2432]{1,0:T(8,128)(2,1)S(1)} %get-tuple-element.12.a_v, bf16[2560,2432]{1,0:T(8,128)(2,1)S(1)} %get-tuple-element.13.b_v.up, f32[2,1,2432]{2,1,0:T(1,128)S(1)} %get-tuple-element.14.fac), custom_call_target="tpu_custom_call" | custom-call | tf_op jit(solution)/shard_map/write_out/pallas_call | solution.py:486
  102.0 5.8 %tail_gather.1.tail = bf16[8,192,2432]{2,1,0:T(8,128)(2,1)S(1)} custom-call(bf16[2560,2432]{1,0:T(8,128)(2,1)S(1)} %get-tuple-element.13.b_v.up, f32[8,128]{1,0:T(8,128)S(1)} %get-tuple-element.16.after), custom_call_target="tpu_custom_call" | custom-call | tf_op jit(solution)/shard_map/tail_gather/pallas_call | solution.py:496
  107.8 2.6 %finish.1 = bf16[2560,2432]{1,0:T(8,128)(2,1)} custom-call(bf16[8,192,2432]{2,1,0:T(8,128)(2,1)S(1)} %tail_gather.1.tail, bf16[2560,2432]{1,0:T(8,128)(2,1)} %get-tuple-element.17.before), custom_call_target="tpu_custom_call", output_to_operand_aliasing={{}: (1, {})} | custom-call | tf_op jit(solution)/shard_map/finish/pallas_call | solution.py:511

commit v5 on v4

--- a/solution.py
+++ b/solution.py
@@ -68,7 +68,7 @@
     out_g, out_u, fac,
     w_v, l_v, h_v, gain_v, low_v, g_v, col_v, part, mine, heard, rf_v,
     raw_v, far_l, far_g, far_low, far_col,
-    in_sem, small_send, small_recv, send, recv,
+    in_sem, small_send, small_recv, sent, crossed, recv,
 ):
     rows, cols = wg_hbm.shape
     me, core, sib, to_x, to_y, diag, flip = place()
@@ -81,7 +81,8 @@
     own_tail = (1, shared_up, solo)
     block = (0, 0, early)
     every = raws + bulk
-    order = {c: i for i, c in enumerate(every + alone + [block, own_tail])}
+    order = {c: i for i, c in enumerate(every + alone)}
+    lanes = {0: 0, 1: 1, 5: 2}
     outs = (out_g, out_u)
 
     barrier = pltpu.get_barrier_semaphore()
@@ -115,11 +116,23 @@
         started.append(c)
         c.start()
 
+    def go(c):
+        c.start()
+
     def remote(src, dst, slot, chunk, target):
-        i = order[chunk]
+        if slot in lanes:
+            got = recv.at[lanes[slot], order[chunk]]
+            out = sent.at[1 if chunk in alone else 0]
+        else:
+            got, out = crossed, sent.at[2]
         return pltpu.make_async_remote_copy(
-            src_ref=src, dst_ref=dst, send_sem=send.at[slot, i],
-            recv_sem=recv.at[slot, i], device_id={AXIS: target})
+            src_ref=src, dst_ref=dst, send_sem=out, recv_sem=got, device_id={AXIS: target})
+
+    def all_of(count, out):
+        part = out_g.at[0:count, :]
+        return pltpu.make_async_remote_copy(
+            src_ref=part, dst_ref=part, send_sem=sent.at[out], recv_sem=crossed,
+            device_id={AXIS: sib})
 
     def small(src, dst, i, target):
         return pltpu.make_async_remote_copy(
@@ -142,8 +155,8 @@
     pl.semaphore_wait(barrier, 3)
     for c, chunk in list(zip(raw_loads, raws))[:2]:
         c.wait()
-        keep(raw_move(0, chunk, 0, to_x))
-        keep(raw_move(1, chunk, 0, to_y))
+        go(raw_move(0, chunk, 0, to_x))
+        go(raw_move(1, chunk, 0, to_y))
     low_own, gain_own = l_v.at[0, :, :early], gain_v.at[:, :early]
     low_loads[0].wait()
     gain_load.wait()
@@ -200,9 +213,6 @@
         mine[2] = mine[1] + heard[2]
         sum_all.start()
 
-    for chunk in raws[2:]:
-        started.append(raw_move(0, chunk, 0, to_x))
-        started.append(raw_move(1, chunk, 0, to_y))
     for a in range(2):
         factor = jnp.sqrt(mine[2, a])
         fac[a] = factor
@@ -214,9 +224,9 @@
         outs[a][r, :] = (g_v[a, s:s + z, :] * rf_v[a]).astype(jnp.bfloat16)
 
     def send_own(chunk):
-        keep(move(0, chunk, me, to_x))
-        keep(move(1, chunk, me, to_y))
-        keep(move(2, chunk, me, sib))
+        go(move(0, chunk, me, to_x))
+        go(move(1, chunk, me, to_y))
+        go(move(2, chunk, me, sib))
 
     for i, chunk in enumerate(bulk):
         scale(chunk)
@@ -226,8 +236,8 @@
     send_own(bulk[-1])
     for chunk in alone:
         scale(chunk)
-    keep(move(2, block, me, sib))
-    keep(move(2, own_tail, me, sib))
+    go(move(2, block, me, sib))
+    go(move(2, own_tail, me, sib))
 
     low_x, low_y = (small(low_own, far_l.at[i], 4 + i, to_x) for i in range(2))
     gain_x, gain_y = (small(gain_own, far_g.at[i], 7 + i, to_x) for i in range(2))
@@ -251,30 +261,30 @@
     for i, chunk in enumerate(raws):
         raw_move(0, chunk, 0, to_x).wait_recv()
         if i % 2 == 0:
-            keep(raw_move(5, chunk, 0, to_y))
+            go(raw_move(5, chunk, 0, to_y))
         raw_move(1, chunk, 0, to_y).wait_recv()
         if i % 2 == 1:
-            keep(raw_move(5, chunk, 1, to_x))
+            go(raw_move(5, chunk, 1, to_x))
     correct(0, to_x)
     correct(1, to_y)
 
-    def relay(i, chunk, keep, forward):
+    def relay(i, chunk, forward):
         move(0, chunk, to_x, to_x).wait_recv()
         if i % 2 == 0:
-            keep(move(5, chunk, to_x, to_y))
+            go(move(5, chunk, to_x, to_y))
         if forward:
-            keep(move(3, chunk, to_x, sib))
+            go(move(3, chunk, to_x, sib))
         move(1, chunk, to_y, to_y).wait_recv()
         if i % 2 == 1:
-            keep(move(5, chunk, to_y, to_x))
+            go(move(5, chunk, to_y, to_x))
         if forward:
-            keep(move(4, chunk, to_y, sib))
+            go(move(4, chunk, to_y, sib))
 
     for i, chunk in enumerate(bulk):
-        relay(i, chunk, keep, True)
+        relay(i, chunk, True)
         if i == 0:
-            keep(move(3, block, to_x, sib))
-            keep(move(4, block, to_y, sib))
+            go(move(3, block, to_x, sib))
+            go(move(4, block, to_y, sib))
 
     @pl.when(core == late)
     def _():
@@ -289,43 +299,33 @@
     correct(2, diag)
     for i, chunk in enumerate(bulk):
         move(5, chunk, diag, to_x).wait_recv()
-        keep(move(6, chunk, diag, sib))
+        go(move(6, chunk, diag, sib))
         if i == 0:
-            keep(move(6, block, diag, sib))
-    for chunk in [block] + bulk:
-        move(2, chunk, sib, sib).wait_recv()
-        move(3, chunk, to_x + flip, sib).wait_recv()
-        move(4, chunk, to_y + flip, sib).wait_recv()
-        move(6, chunk, diag + flip, sib).wait_recv()
-    move(2, own_tail, sib, sib).wait_recv()
+            go(move(6, block, diag, sib))
+    arrived = 3 * early + sum(3 * z for _, _, z in bulk) + rows + rows
+    all_of(arrived, 2).wait_recv()
 
     @pl.when(core == late)
     def _():
-        own = []
-
-        def go(c):
-            own.append(c)
-            c.start()
-
         for i, chunk in enumerate(alone):
-            relay(i, chunk, go, False)
+            relay(i, chunk, False)
         for chunk in alone:
             move(5, chunk, diag, to_x).wait_recv()
-            move(0, chunk, me, to_x).wait_send()
-            move(1, chunk, me, to_y).wait_send()
-        for c in own + [sum_pair]:
-            c.wait_send()
+        all_of(3 * solo, 1).wait_send()
+        sum_pair.wait_send()
 
     @pl.when(core != late)
     def _():
         for c in (sum_x, sum_y, sum_all):
             c.wait_send()
 
+    all_of(3 * sum(z for _, _, z in every), 0).wait_send()
+    all_of(arrived, 2).wait_send()
     for c in started:
         c.wait_send()
 
 
-def tail_kernel(rows, unit, up, after, tail, ready, send, recv):
+def tail_kernel(rows, unit, up, after, tail, ready, sent, crossed, recv):
     solo = tail.shape[1]
     me, core, sib, to_x, to_y, diag, flip = place()
     chunks = pairs(0, unit, ALONE)
@@ -333,10 +333,19 @@
     rest = (to_x, to_y, diag)
     barrier = pltpu.get_barrier_semaphore()
 
+    lanes = {0: 0, 1: 1, 5: 2}
+
     def remote(src, dst, slot, i, target):
+        inner = slot in lanes
         return pltpu.make_async_remote_copy(
-            src_ref=src, dst_ref=dst, send_sem=send.at[slot, i],
-            recv_sem=recv.at[slot, i], device_id={AXIS: target})
+            src_ref=src, dst_ref=dst, send_sem=sent.at[0 if inner else 1],
+            recv_sem=recv.at[lanes[slot], i] if inner else crossed, device_id={AXIS: target})
+
+    def all_of(out):
+        part = tail.at[0:3]
+        return pltpu.make_async_remote_copy(
+            src_ref=part, dst_ref=part, send_sem=sent.at[out], recv_sem=crossed,
+            device_id={AXIS: sib})
 
     def held(owner, s, z):
         return up.at[pl.ds(pl.multiple_of(owner * rows + rows - solo + s, 8), z), :]
@@ -350,87 +359,77 @@
         r = pl.ds(pl.multiple_of(owner * rows + rows - solo, 8), solo)
         tail[owner] = up[r, :]
 
+    def go(c):
+        c.start()
+
     @pl.when(core != late)
     def _():
-        started = []
-
-        def keep(c):
-            started.append(c)
-            c.start()
-
         for d in (to_x, to_y, sib):
             pl.semaphore_signal(barrier, inc=1, device_id={AXIS: d})
         pl.semaphore_wait(barrier, 2)
         for i, c in enumerate(chunks):
-            keep(move(0, i, c, me, to_x, True))
-            keep(move(1, i, c, me, to_y, True))
+            go(move(0, i, c, me, to_x, True))
+            go(move(1, i, c, me, to_y, True))
         for i, c in enumerate(chunks):
             move(0, i, c, to_x, to_x).wait_recv()
             if i % 2 == 0:
-                keep(move(5, i, c, to_x, to_y))
+                go(move(5, i, c, to_x, to_y))
             move(1, i, c, to_y, to_y).wait_recv()
             if i % 2 == 1:
-                keep(move(5, i, c, to_y, to_x))
+                go(move(5, i, c, to_y, to_x))
         pl.semaphore_wait(ready, 1)
-        keep(move(3, 0, whole, to_x, sib))
-        keep(move(4, 0, whole, to_y, sib))
+        go(move(3, 0, whole, to_x, sib))
+        go(move(4, 0, whole, to_y, sib))
         for i, c in enumerate(chunks):
             move(5, i, c, diag, to_x).wait_recv()
-            keep(move(6, i, c, diag, sib))
-        for i, owner in enumerate(rest):
-            move(7, i, whole, owner + flip, sib).wait_recv()
-        for c in started:
-            c.wait_send()
+            go(move(6, i, c, diag, sib))
+        all_of(0).wait_send()
 
     @pl.when(core == late)
     def _():
         pl.semaphore_wait(barrier, 1)
         pl.semaphore_signal(ready, inc=1, device_id={AXIS: sib})
-        out = [move(7, i, whole, owner, sib, True) for i, owner in enumerate(rest)]
-        for c in out:
-            c.start()
+        for i, owner in enumerate(rest):
+            go(move(7, i, whole, owner, sib, True))
         for owner in rest:
             copy(owner)
-        move(3, 0, whole, to_x + flip, sib).wait_recv()
-        move(4, 0, whole, to_y + flip, sib).wait_recv()
-        for i, c in enumerate(chunks):
-            move(6, i, c, diag + flip, sib).wait_recv()
-        for c in out:
-            c.wait_send()
-
-
-def write_kernel(rows, solo, a_v, b_v, fac, a_hbm, b_hbm, fa_hbm, fb_hbm, done, sem, fac_sem):
+
+    all_of(1).wait_recv()
+    all_of(1).wait_send()
+
+
+def write_kernel(rows, solo, a_v, b_v, fac, a_hbm, b_hbm, fa_hbm, fb_hbm, done, sem):
     done[...] = jnp.zeros_like(done)
     n = a_v.shape[0] // rows
     first = lax.axis_index(AXIS) // 2 * 2
-    copies = [
-        pltpu.make_async_copy(fac.at[i, 0], dst, fac_sem.at[i])
+    waits = [
+        pltpu.make_async_copy(fac.at[i, 0], dst, sem.at[i])
         for i, dst in enumerate((fa_hbm, fb_hbm))
     ]
+    for c in waits:
+        c.start()
     for k in range(n):
         for i, (src, dst) in enumerate(((a_v, a_hbm), (b_v, b_hbm))):
             owner = lax.rem(first + k, n)
             z = rows - solo if i and k > 1 else rows
             r = pl.ds(pl.multiple_of(owner * rows, 8), z)
-            copies.append(pltpu.make_async_copy(src.at[r, :], dst.at[r, :], sem.at[i, k]))
-    for c in copies:
-        c.start()
-    for c in copies:
+            pltpu.make_async_copy(src.at[r, :], dst.at[r, :], sem.at[2 + i]).start()
+    waits.append(pltpu.make_async_copy(a_v, a_hbm, sem.at[2]))
+    r = pl.ds(0, n * rows - (n - 2) * solo)
+    waits.append(pltpu.make_async_copy(b_v.at[r, :], b_hbm.at[r, :], sem.at[3]))
+    for c in waits:
         c.wait()
 
 
 def finish_kernel(rows, tail, before, b_hbm, sem):
     n, solo, _ = tail.shape
     first = lax.axis_index(AXIS) // 2 * 2
-    copies = []
     for k in range(2, n):
         owner = lax.rem(first + k, n)
         r = pl.ds(pl.multiple_of((owner + 1) * rows - solo, 8), solo)
-        copies.append(pltpu.make_async_copy(tail.at[owner], b_hbm.at[r, :], sem.at[k]))
-    for c in copies:
-        c.start()
-    for c in copies:
-        c.wait()
+        pltpu.make_async_copy(tail.at[owner], b_hbm.at[r, :], sem).start()
+    part = b_hbm.at[0:(n - 2) * solo, :]
+    pltpu.make_async_copy(part, part, sem).wait()
 
 
 def paired(n, weight_gate, low_gate, high_gate, weight_up, low_up, high_up, norm_gain):
@@ -444,7 +443,7 @@
     space = pl.BlockSpec(memory_space=pltpu.HBM)
     rank = high_gate.shape[0]
     grant = 65472 * 2**10 - (4 * full[0] * cols + 8 * cols) // 2**10 * 2**10 - 24 * 2**10
-    slots = 20
+    moves = 2 * (len(RAW) + len(GATE) + len(UP) + len(ALONE))
     gate, up, fac = pl.pallas_call(
         functools.partial(gather_kernel, unit, solo),
         out_shape=(
@@ -474,8 +473,9 @@
             pltpu.SemaphoreType.DMA((7 + 2 * len(RAW),)),
             pltpu.SemaphoreType.DMA((10,)),
             pltpu.SemaphoreType.DMA((10,)),
-            pltpu.SemaphoreType.DMA((7, slots)),
-            pltpu.SemaphoreType.DMA((7, slots)),
+            pltpu.SemaphoreType.DMA((3,)),
+            pltpu.SemaphoreType.DMA,
+            pltpu.SemaphoreType.DMA((3, moves)),
         ],
         compiler_params=pltpu.CompilerParams(
             collective_id=0, has_side_effects=True, vmem_limit_bytes=grant
@@ -489,7 +489,7 @@
         + (pltpu.VMEM((8, 128), jnp.float32),),
         in_specs=[vmem, vmem, vmem],
         out_specs=(hbm,) * 4 + (vmem,),
-        scratch_shapes=[pltpu.SemaphoreType.DMA((2, n)), pltpu.SemaphoreType.DMA((2,))],
+        scratch_shapes=[pltpu.SemaphoreType.DMA((4,))],
         compiler_params=pltpu.CompilerParams(vmem_limit_bytes=2**20),
         name="write_out",
     )(gate, up, fac)
@@ -500,8 +500,9 @@
         out_specs=vmem,
         scratch_shapes=[
             pltpu.SemaphoreType.REGULAR,
-            pltpu.SemaphoreType.DMA((8, 2 * len(ALONE))),
-            pltpu.SemaphoreType.DMA((8, 2 * len(ALONE))),
+            pltpu.SemaphoreType.DMA((2,)),
+            pltpu.SemaphoreType.DMA,
+            pltpu.SemaphoreType.DMA((3, 2 * len(ALONE))),
         ],
         compiler_params=pltpu.CompilerParams(
             collective_id=1, has_side_effects=True, vmem_limit_bytes=2**20
@@ -514,7 +515,7 @@
         in_specs=[vmem, hbm],
         out_specs=hbm,
         input_output_aliases={1: 0},
-        scratch_shapes=[pltpu.SemaphoreType.DMA((n,))],
+        scratch_shapes=[pltpu.SemaphoreType.DMA],
         compiler_params=pltpu.CompilerParams(vmem_limit_bytes=2**20),
         name="finish",
     )(tail, ready_up)

time: 110 us -> 110 us (level)
  no operation moved by 1% of the time
where the time goes in v5:
time: 110 us
  Pallas kernels  109 us (99%)
    pallas_call x1, Pallas kernels, paired(): pl.pallas_call(functools.partial(gather_kernel, unit, solo), out_shape=(p...  94.7 us
    pallas_call x1, Pallas kernels, paired(): pl.pallas_call(functools.partial(write_kernel, rows, solo), out_shape=(wh...  6.63 us
    pallas_call x1, Pallas kernels, paired(): pl.pallas_call(functools.partial(tail_kernel, rows, unit), out_shape=pltp...  5.37 us
    pallas_call x1, Pallas kernels, paired(): pl.pallas_call(functools.partial(finish_kernel, rows), out_shape=whole, i...  2.5 us

profile of v5, /device:TPU:0, one launch (start us, length us, event | category | flops | bytes accessed | tf_op | source)
XLA Modules:
  0.0 109.8 jit_solution(1480980036383299842)
XLA Ops:
  0.6 94.7 %merge_gather.1 = (bf16[2560,2432]{1,0:T(8,128)(2,1)S(1)}, bf16[2560,2432]{1,0:T(8,128)(2,1)S(1)}, f32[2,1,2432]{2,1,0:T(1,128)S(1)}) custom-call(bf16[320,2432]{1,0:T(8,128)(2,1)} %wg_hbm.1, bf16[320,2432]{1,0:T(8,128)(2,1)} %wu_hbm.1, bf16[32,320]{1,0:T(8,128)(2,1)} %bitcast.2, bf16[32,320]{1,0:T(8,128)(2,1)} %bitcast.3, bf16[32,2432]{1,0:T(8,128)(2,1)} %hg_hbm.1, ...), custom_call_target="tpu_custom_call" | custom-call | tf_op jit(solution)/shard_map/merge_gather/pallas_call | solution.py:447
  95.3 6.6 %write_out.1 = (bf16[2560,2432]{1,0:T(8,128)(2,1)}, bf16[2560,2432]{1,0:T(8,128)(2,1)}, f32[2432]{0:T(1024)}, f32[2432]{0:T(1024)}, f32[8,128]{1,0:T(8,128)S(1)}) custom-call(bf16[2560,2432]{1,0:T(8,128)(2,1)S(1)} %get-tuple-element.12.a_v, bf16[2560,2432]{1,0:T(8,128)(2,1)S(1)} %get-tuple-element.13.b_v.up, f32[2,1,2432]{2,1,0:T(1,128)S(1)} %get-tuple-element.14.fac), custom_call_target="tpu_custom_call" | custom-call | tf_op jit(solution)/shard_map/write_out/pallas_call | solution.py:486
  102.0 5.4 %tail_gather.1.tail = bf16[8,192,2432]{2,1,0:T(8,128)(2,1)S(1)} custom-call(bf16[2560,2432]{1,0:T(8,128)(2,1)S(1)} %get-tuple-element.13.b_v.up, f32[8,128]{1,0:T(8,128)S(1)} %get-tuple-element.16.after), custom_call_target="tpu_custom_call" | custom-call | tf_op jit(solution)/shard_map/tail_gather/pallas_call | solution.py:496
  107.3 2.5 %finish.1 = bf16[2560,2432]{1,0:T(8,128)(2,1)} custom-call(bf16[8,192,2432]{2,1,0:T(8,128)(2,1)S(1)} %tail_gather.1.tail, bf16[2560,2432]{1,0:T(8,128)(2,1)} %get-tuple-element.17.before), custom_call_target="tpu_custom_call", output_to_operand_aliasing={{}: (1, {})} | custom-call | tf_op jit(solution)/shard_map/finish/pallas_call | solution.py:512

commit v6 on v5

--- a/solution.py
+++ b/solution.py
@@ -40,8 +40,8 @@
 late = 0
 RAW = (4, 4)
 GATE = (12,)
-UP = (4, 4)
-ALONE = (8, 4)
+UP = (10,)
+ALONE = (7, 3)
 
 
 def place():
@@ -355,10 +355,6 @@
         dst = tail.at[owner, s:s + z, :]
         return remote(held(owner, s, z) if first else dst, dst, slot, i, target)
 
-    def copy(owner):
-        r = pl.ds(pl.multiple_of(owner * rows + rows - solo, 8), solo)
-        tail[owner] = up[r, :]
-
     def go(c):
         c.start()
 
@@ -391,8 +387,6 @@
         pl.semaphore_signal(ready, inc=1, device_id={AXIS: sib})
         for i, owner in enumerate(rest):
             go(move(7, i, whole, owner, sib, True))
-        for owner in rest:
-            copy(owner)
 
     all_of(1).wait_recv()
     all_of(1).wait_send()
@@ -414,22 +408,51 @@
             z = rows - solo if i and k > 1 else rows
             r = pl.ds(pl.multiple_of(owner * rows, 8), z)
             pltpu.make_async_copy(src.at[r, :], dst.at[r, :], sem.at[2 + i]).start()
+    me = lax.axis_index(AXIS)
+    alone = lax.rem(me, 2) == late
+
+    @pl.when(alone)
+    def _():
+        for k in range(2, n, 2):
+            r = pl.ds(pl.multiple_of((lax.rem(me + k, n) + 1) * rows - solo, 8), solo)
+            pltpu.make_async_copy(b_v.at[r, :], b_hbm.at[r, :], sem.at[4]).start()
+
     waits.append(pltpu.make_async_copy(a_v, a_hbm, sem.at[2]))
     r = pl.ds(0, n * rows - (n - 2) * solo)
     waits.append(pltpu.make_async_copy(b_v.at[r, :], b_hbm.at[r, :], sem.at[3]))
     for c in waits:
         c.wait()
 
+    @pl.when(alone)
+    def _():
+        part = b_hbm.at[0:(n // 2 - 1) * solo, :]
+        pltpu.make_async_copy(part, part, sem.at[4]).wait()
+
 
 def finish_kernel(rows, tail, before, b_hbm, sem):
     n, solo, _ = tail.shape
-    first = lax.axis_index(AXIS) // 2 * 2
-    for k in range(2, n):
-        owner = lax.rem(first + k, n)
-        r = pl.ds(pl.multiple_of((owner + 1) * rows - solo, 8), solo)
-        pltpu.make_async_copy(tail.at[owner], b_hbm.at[r, :], sem).start()
-    part = b_hbm.at[0:(n - 2) * solo, :]
-    pltpu.make_async_copy(part, part, sem).wait()
+    me = lax.axis_index(AXIS)
+    first = me // 2 * 2
+    part = b_hbm.at[0:(n // 2 - 1) * solo, :]
+
+    def write(side):
+        for k in range(2, n, 2):
+            owner = lax.rem(first + k + side, n)
+            r = pl.ds(pl.multiple_of((owner + 1) * rows - solo, 8), solo)
+            pltpu.make_async_copy(tail.at[owner], b_hbm.at[r, :], sem.at[side]).start()
+
+    def wait(side):
+        pltpu.make_async_copy(part, part, sem.at[side]).wait()
+
+    write(1 - late)
+    own = lax.rem(me, 2) == late
+
+    @pl.when(jnp.logical_not(own))
+    def _():
+        write(late)
+        wait(late)
+
+    wait(1 - late)
 
 
 def paired(n, weight_gate, low_gate, high_gate, weight_up, low_up, high_up, norm_gain):
@@ -489,7 +512,7 @@
         + (pltpu.VMEM((8, 128), jnp.float32),),
         in_specs=[vmem, vmem, vmem],
         out_specs=(hbm,) * 4 + (vmem,),
-        scratch_shapes=[pltpu.SemaphoreType.DMA((4,))],
+        scratch_shapes=[pltpu.SemaphoreType.DMA((5,))],
         compiler_params=pltpu.CompilerParams(vmem_limit_bytes=2**20),
         name="write_out",
     )(gate, up, fac)
@@ -515,7 +538,7 @@
         in_specs=[vmem, hbm],
         out_specs=hbm,
         input_output_aliases={1: 0},
-        scratch_shapes=[pltpu.SemaphoreType.DMA],
+        scratch_shapes=[pltpu.SemaphoreType.DMA((2,))],
         compiler_params=pltpu.CompilerParams(vmem_limit_bytes=2**20),
         name="finish",
     )(tail, ready_up)

time: 110 us -> 109 us (level)
  no operation moved by 1% of the time
where the time goes in v6:
time: 109 us
  Pallas kernels  108 us (99%)
    pallas_call x1, Pallas kernels, paired(): pl.pallas_call(functools.partial(gather_kernel, unit, solo), out_shape=(p...  94.2 us
    pallas_call x1, Pallas kernels, paired(): pl.pallas_call(functools.partial(write_kernel, rows, solo), out_shape=(wh...  7.63 us
    pallas_call x1, Pallas kernels, paired(): pl.pallas_call(functools.partial(tail_kernel, rows, unit), out_shape=pltp...  4.77 us

profile of v6, /device:TPU:0, one launch (start us, length us, event | category | flops | bytes accessed | tf_op | source)
XLA Modules:
  0.0 108.7 jit_solution(11927441311899753491)
XLA Ops:
  0.6 94.2 %merge_gather.1 = (bf16[2560,2432]{1,0:T(8,128)(2,1)S(1)}, bf16[2560,2432]{1,0:T(8,128)(2,1)S(1)}, f32[2,1,2432]{2,1,0:T(1,128)S(1)}) custom-call(bf16[320,2432]{1,0:T(8,128)(2,1)} %wg_hbm.1, bf16[320,2432]{1,0:T(8,128)(2,1)} %wu_hbm.1, bf16[32,320]{1,0:T(8,128)(2,1)} %bitcast.2, bf16[32,320]{1,0:T(8,128)(2,1)} %bitcast.3, bf16[32,2432]{1,0:T(8,128)(2,1)} %hg_hbm.1, ...), custom_call_target="tpu_custom_call" | custom-call | tf_op jit(solution)/shard_map/merge_gather/pallas_call | solution.py:470
  94.8 7.6 %write_out.1 = (bf16[2560,2432]{1,0:T(8,128)(2,1)}, bf16[2560,2432]{1,0:T(8,128)(2,1)}, f32[2432]{0:T(1024)}, f32[2432]{0:T(1024)}, f32[8,128]{1,0:T(8,128)S(1)}) custom-call(bf16[2560,2432]{1,0:T(8,128)(2,1)S(1)} %get-tuple-element.12.a_v, bf16[2560,2432]{1,0:T(8,128)(2,1)S(1)} %get-tuple-element.13.b_v.up, f32[2,1,2432]{2,1,0:T(1,128)S(1)} %get-tuple-element.14.fac), custom_call_target="tpu_custom_call" | custom-call | tf_op jit(solution)/shard_map/write_out/pallas_call | solution.py:509
  102.5 4.8 %tail_gather.1.tail = bf16[8,160,2432]{2,1,0:T(8,128)(2,1)S(1)} custom-call(bf16[2560,2432]{1,0:T(8,128)(2,1)S(1)} %get-tuple-element.13.b_v.up, f32[8,128]{1,0:T(8,128)S(1)} %get-tuple-element.16.after), custom_call_target="tpu_custom_call" | custom-call | tf_op jit(solution)/shard_map/tail_gather/pallas_call | solution.py:519
  107.3 1.4 %finish.1 = bf16[2560,2432]{1,0:T(8,128)(2,1)} custom-call(bf16[8,160,2432]{2,1,0:T(8,128)(2,1)S(1)} %tail_gather.1.tail, bf16[2560,2432]{1,0:T(8,128)(2,1)} %get-tuple-element.17.before), custom_call_target="tpu_custom_call", output_to_operand_aliasing={{}: (1, {})} | custom-call | tf_op jit(solution)/shard_map/finish/pallas_call | solution.py:535

commit v7 on v6

--- a/solution.py
+++ b/solution.py
@@ -41,7 +41,7 @@
 RAW = (4, 4)
 GATE = (12,)
 UP = (10,)
-ALONE = (7, 3)
+ALONE = (5, 3, 2)
 
 
 def place():
@@ -241,12 +241,11 @@
 
     low_x, low_y = (small(low_own, far_l.at[i], 4 + i, to_x) for i in range(2))
     gain_x, gain_y = (small(gain_own, far_g.at[i], 7 + i, to_x) for i in range(2))
-    low_x.wait_recv()
-    keep(small(far_l.at[0], far_l.at[2], 6, to_y))
-    gain_x.wait_recv()
-    keep(small(far_g.at[0], far_g.at[2], 9, to_y))
-    low_y.wait_recv()
-    gain_y.wait_recv()
+    for c in (low_x, low_y, gain_x, gain_y):
+        c.wait_recv()
+    over = to_y + core * (to_x - to_y)
+    keep(small(far_l.at[core], far_l.at[2], 6, over))
+    keep(small(far_g.at[core], far_g.at[2], 9, over))
 
     def correct(i, owner):
         far_low[i] = (mix_rate * far_l[i].astype(jnp.float32)).T.astype(jnp.bfloat16)

time: 109 us -> 109 us (level)
  no operation moved by 1% of the time
where the time goes in v7:
time: 109 us
  Pallas kernels  108 us (99%)
    pallas_call x1, Pallas kernels, paired(): pl.pallas_call(functools.partial(gather_kernel, unit, solo), out_shape=(p...  93.7 us
    pallas_call x1, Pallas kernels, paired(): pl.pallas_call(functools.partial(write_kernel, rows, solo), out_shape=(wh...  7.63 us
    pallas_call x1, Pallas kernels, paired(): pl.pallas_call(functools.partial(tail_kernel, rows, unit), out_shape=pltp...  5.11 us

profile of v7, /device:TPU:0, one launch (start us, length us, event | category | flops | bytes accessed | tf_op | source)
XLA Modules:
  0.0 108.5 jit_solution(15188751331411355832)
XLA Ops:
  0.6 93.7 %merge_gather.1 = (bf16[2560,2432]{1,0:T(8,128)(2,1)S(1)}, bf16[2560,2432]{1,0:T(8,128)(2,1)S(1)}, f32[2,1,2432]{2,1,0:T(1,128)S(1)}) custom-call(bf16[320,2432]{1,0:T(8,128)(2,1)} %wg_hbm.1, bf16[320,2432]{1,0:T(8,128)(2,1)} %wu_hbm.1, bf16[32,320]{1,0:T(8,128)(2,1)} %bitcast.2, bf16[32,320]{1,0:T(8,128)(2,1)} %bitcast.3, bf16[32,2432]{1,0:T(8,128)(2,1)} %hg_hbm.1, ...), custom_call_target="tpu_custom_call" | custom-call | tf_op jit(solution)/shard_map/merge_gather/pallas_call | solution.py:469
  94.3 7.6 %write_out.1 = (bf16[2560,2432]{1,0:T(8,128)(2,1)}, bf16[2560,2432]{1,0:T(8,128)(2,1)}, f32[2432]{0:T(1024)}, f32[2432]{0:T(1024)}, f32[8,128]{1,0:T(8,128)S(1)}) custom-call(bf16[2560,2432]{1,0:T(8,128)(2,1)S(1)} %get-tuple-element.12.a_v, bf16[2560,2432]{1,0:T(8,128)(2,1)S(1)} %get-tuple-element.13.b_v.up, f32[2,1,2432]{2,1,0:T(1,128)S(1)} %get-tuple-element.14.fac), custom_call_target="tpu_custom_call" | custom-call | tf_op jit(solution)/shard_map/write_out/pallas_call | solution.py:508
  102.0 5.1 %tail_gather.1.tail = bf16[8,160,2432]{2,1,0:T(8,128)(2,1)S(1)} custom-call(bf16[2560,2432]{1,0:T(8,128)(2,1)S(1)} %get-tuple-element.13.b_v.up, f32[8,128]{1,0:T(8,128)S(1)} %get-tuple-element.16.after), custom_call_target="tpu_custom_call" | custom-call | tf_op jit(solution)/shard_map/tail_gather/pallas_call | solution.py:518
  107.1 1.4 %finish.1 = bf16[2560,2432]{1,0:T(8,128)(2,1)} custom-call(bf16[8,160,2432]{2,1,0:T(8,128)(2,1)S(1)} %tail_gather.1.tail, bf16[2560,2432]{1,0:T(8,128)(2,1)} %get-tuple-element.17.before), custom_call_target="tpu_custom_call", output_to_operand_aliasing={{}: (1, {})} | custom-call | tf_op jit(solution)/shard_map/finish/pallas_call | solution.py:534

commit v8 on v7

--- a/solution.py
+++ b/solution.py
@@ -38,7 +38,7 @@
 
 
 late = 0
-RAW = (4, 4)
+RAW = (2, 6)
 GATE = (12,)
 UP = (10,)
 ALONE = (5, 3, 2)
@@ -110,12 +110,6 @@
     for c in (loads[0], low_loads[1], high_loads[1], loads[1]):
         c.start()
 
-    started = []
-
-    def keep(c):
-        started.append(c)
-        c.start()
-
     def go(c):
         c.start()
 
@@ -136,7 +130,7 @@
 
     def small(src, dst, i, target):
         return pltpu.make_async_remote_copy(
-            src_ref=src, dst_ref=dst, send_sem=small_send.at[i],
+            src_ref=src, dst_ref=dst, send_sem=small_send.at[(i >= 4) + (i >= 7)],
             recv_sem=small_recv.at[i], device_id={AXIS: target})
 
     def piece(chunk, owner):
@@ -161,8 +155,8 @@
     low_loads[0].wait()
     gain_load.wait()
     for i, d in enumerate((to_x, to_y)):
-        keep(small(low_own, far_l.at[i], 4 + i, d))
-        keep(small(gain_own, far_g.at[i], 7 + i, d))
+        go(small(low_own, far_l.at[i], 4 + i, d))
+        go(small(gain_own, far_g.at[i], 7 + i, d))
 
     col_v[...] = jnp.broadcast_to(gain_v[...], (128, rows)).T
     step = rows // 5
@@ -244,8 +238,8 @@
     for c in (low_x, low_y, gain_x, gain_y):
         c.wait_recv()
     over = to_y + core * (to_x - to_y)
-    keep(small(far_l.at[core], far_l.at[2], 6, over))
-    keep(small(far_g.at[core], far_g.at[2], 9, over))
+    go(small(far_l.at[core], far_l.at[2], 6, over))
+    go(small(far_g.at[core], far_g.at[2], 9, over))
 
     def correct(i, owner):
         far_low[i] = (mix_rate * far_l[i].astype(jnp.float32)).T.astype(jnp.bfloat16)
@@ -285,12 +279,6 @@
             go(move(3, block, to_x, sib))
             go(move(4, block, to_y, sib))
 
-    @pl.when(core == late)
-    def _():
-        for chunk in alone:
-            move(0, chunk, me, to_x).start()
-            move(1, chunk, me, to_y).start()
-
     for chunk in raws:
         raw_move(5, chunk, 0, to_x).wait_recv()
     small(far_l.at[0], far_l.at[2], 6, to_y).wait_recv()
@@ -301,6 +289,12 @@
         go(move(6, chunk, diag, sib))
         if i == 0:
             go(move(6, block, diag, sib))
+        if i == 0:
+            @pl.when(core == late)
+            def _():
+                for chunk in alone:
+                    move(0, chunk, me, to_x).start()
+                    move(1, chunk, me, to_y).start()
     arrived = 3 * early + sum(3 * z for _, _, z in bulk) + rows + rows
     all_of(arrived, 2).wait_recv()
 
@@ -315,13 +309,12 @@
 
     @pl.when(core != late)
     def _():
-        for c in (sum_x, sum_y, sum_all):
-            c.wait_send()
+        small(heard, heard, 0, sib).wait_send()
 
     all_of(3 * sum(z for _, _, z in every), 0).wait_send()
     all_of(arrived, 2).wait_send()
-    for c in started:
-        c.wait_send()
+    small(far_l, far_l, 4, to_x).wait_send()
+    small(far_g, far_g, 7, to_x).wait_send()
 
 
 def tail_kernel(rows, unit, up, after, tail, ready, sent, crossed, recv):
@@ -493,7 +486,7 @@
             pltpu.VMEM((3, early, rank), jnp.bfloat16),
             pltpu.VMEM((3, early, 128), jnp.float32),
             pltpu.SemaphoreType.DMA((7 + 2 * len(RAW),)),
-            pltpu.SemaphoreType.DMA((10,)),
+            pltpu.SemaphoreType.DMA((3,)),
             pltpu.SemaphoreType.DMA((10,)),
             pltpu.SemaphoreType.DMA((3,)),
             pltpu.SemaphoreType.DMA,

time: 109 us -> 109 us (level)
  no operation moved by 1% of the time
where the time goes in v8:
time: 109 us; the launch traced here: 108 us
  Pallas kernels  108 us (99%)
    pallas_call x1, Pallas kernels, paired(): pl.pallas_call(functools.partial(gather_kernel, unit, solo), out_shape=(p...  93.6 us
    pallas_call x1, Pallas kernels, paired(): pl.pallas_call(functools.partial(write_kernel, rows, solo), out_shape=(wh...  7.63 us
    pallas_call x1, Pallas kernels, paired(): pl.pallas_call(functools.partial(tail_kernel, rows, unit), out_shape=pltp...  5.1 us

profile of v8, /device:TPU:0, one launch (start us, length us, event | category | flops | bytes accessed | tf_op | source)
XLA Modules:
  0.0 108.5 jit_solution(14867496424942913490)
XLA Ops:
  0.6 93.6 %merge_gather.1 = (bf16[2560,2432]{1,0:T(8,128)(2,1)S(1)}, bf16[2560,2432]{1,0:T(8,128)(2,1)S(1)}, f32[2,1,2432]{2,1,0:T(1,128)S(1)}) custom-call(bf16[320,2432]{1,0:T(8,128)(2,1)} %wg_hbm.1, bf16[320,2432]{1,0:T(8,128)(2,1)} %wu_hbm.1, bf16[32,320]{1,0:T(8,128)(2,1)} %bitcast.2, bf16[32,320]{1,0:T(8,128)(2,1)} %bitcast.3, bf16[32,2432]{1,0:T(8,128)(2,1)} %hg_hbm.1, ...), custom_call_target="tpu_custom_call" | custom-call | tf_op jit(solution)/shard_map/merge_gather/pallas_call | solution.py:462
  94.3 7.6 %write_out.1 = (bf16[2560,2432]{1,0:T(8,128)(2,1)}, bf16[2560,2432]{1,0:T(8,128)(2,1)}, f32[2432]{0:T(1024)}, f32[2432]{0:T(1024)}, f32[8,128]{1,0:T(8,128)S(1)}) custom-call(bf16[2560,2432]{1,0:T(8,128)(2,1)S(1)} %get-tuple-element.12.a_v, bf16[2560,2432]{1,0:T(8,128)(2,1)S(1)} %get-tuple-element.13.b_v.up, f32[2,1,2432]{2,1,0:T(1,128)S(1)} %get-tuple-element.14.fac), custom_call_target="tpu_custom_call" | custom-call | tf_op jit(solution)/shard_map/write_out/pallas_call | solution.py:501
  101.9 5.1 %tail_gather.1.tail = bf16[8,160,2432]{2,1,0:T(8,128)(2,1)S(1)} custom-call(bf16[2560,2432]{1,0:T(8,128)(2,1)S(1)} %get-tuple-element.13.b_v.up, f32[8,128]{1,0:T(8,128)S(1)} %get-tuple-element.16.after), custom_call_target="tpu_custom_call" | custom-call | tf_op jit(solution)/shard_map/tail_gather/pallas_call | solution.py:511
  107.0 1.4 %finish.1 = bf16[2560,2432]{1,0:T(8,128)(2,1)} custom-call(bf16[8,160,2432]{2,1,0:T(8,128)(2,1)S(1)} %tail_gather.1.tail, bf16[2560,2432]{1,0:T(8,128)(2,1)} %get-tuple-element.17.before), custom_call_target="tpu_custom_call", output_to_operand_aliasing={{}: (1, {})} | custom-call | tf_op jit(solution)/shard_map/finish/pallas_call | solution.py:527

commit v9 on v8

--- a/solution.py
+++ b/solution.py
@@ -41,7 +41,7 @@
 RAW = (2, 6)
 GATE = (12,)
 UP = (10,)
-ALONE = (5, 3, 2)
+ALONE = (4, 4, 2)
 
 
 def place():

time: 109 us -> 109 us (level)
  no operation moved by 1% of the time
where the time goes in v9:
time: 109 us; the launch traced here: 108 us
  Pallas kernels  108 us (99%)
    pallas_call x1, Pallas kernels, paired(): pl.pallas_call(functools.partial(gather_kernel, unit, solo), out_shape=(p...  93.6 us
    pallas_call x1, Pallas kernels, paired(): pl.pallas_call(functools.partial(write_kernel, rows, solo), out_shape=(wh...  7.63 us
    pallas_call x1, Pallas kernels, paired(): pl.pallas_call(functools.partial(tail_kernel, rows, unit), out_shape=pltp...  5.1 us

profile of v9, /device:TPU:0, one launch (start us, length us, event | category | flops | bytes accessed | tf_op | source)
XLA Modules:
  0.0 108.5 jit_solution(5455335398823848664)
XLA Ops:
  0.6 93.6 %merge_gather.1 = (bf16[2560,2432]{1,0:T(8,128)(2,1)S(1)}, bf16[2560,2432]{1,0:T(8,128)(2,1)S(1)}, f32[2,1,2432]{2,1,0:T(1,128)S(1)}) custom-call(bf16[320,2432]{1,0:T(8,128)(2,1)} %wg_hbm.1, bf16[320,2432]{1,0:T(8,128)(2,1)} %wu_hbm.1, bf16[32,320]{1,0:T(8,128)(2,1)} %bitcast.2, bf16[32,320]{1,0:T(8,128)(2,1)} %bitcast.3, bf16[32,2432]{1,0:T(8,128)(2,1)} %hg_hbm.1, ...), custom_call_target="tpu_custom_call" | custom-call | tf_op jit(solution)/shard_map/merge_gather/pallas_call | solution.py:462
  94.3 7.6 %write_out.1 = (bf16[2560,2432]{1,0:T(8,128)(2,1)}, bf16[2560,2432]{1,0:T(8,128)(2,1)}, f32[2432]{0:T(1024)}, f32[2432]{0:T(1024)}, f32[8,128]{1,0:T(8,128)S(1)}) custom-call(bf16[2560,2432]{1,0:T(8,128)(2,1)S(1)} %get-tuple-element.12.a_v, bf16[2560,2432]{1,0:T(8,128)(2,1)S(1)} %get-tuple-element.13.b_v.up, f32[2,1,2432]{2,1,0:T(1,128)S(1)} %get-tuple-element.14.fac), custom_call_target="tpu_custom_call" | custom-call | tf_op jit(solution)/shard_map/write_out/pallas_call | solution.py:501
  101.9 5.1 %tail_gather.1.tail = bf16[8,160,2432]{2,1,0:T(8,128)(2,1)S(1)} custom-call(bf16[2560,2432]{1,0:T(8,128)(2,1)S(1)} %get-tuple-element.13.b_v.up, f32[8,128]{1,0:T(8,128)S(1)} %get-tuple-element.16.after), custom_call_target="tpu_custom_call" | custom-call | tf_op jit(solution)/shard_map/tail_gather/pallas_call | solution.py:511
  107.0 1.4 %finish.1 = bf16[2560,2432]{1,0:T(8,128)(2,1)} custom-call(bf16[8,160,2432]{2,1,0:T(8,128)(2,1)S(1)} %tail_gather.1.tail, bf16[2560,2432]{1,0:T(8,128)(2,1)} %get-tuple-element.17.before), custom_call_target="tpu_custom_call", output_to_operand_aliasing={{}: (1, {})} | custom-call | tf_op jit(solution)/shard_map/finish/pallas_call | solution.py:527
